TPU v7x, 64 devices: a 2x2x8 block of a 4x4x8 slice. The times are simulated.
64 devices in a mesh: rep: 4 (over x, y), dp: 16 (over z, core).
Axes of the slice: x: 2, y: 2, z: 8, core: 2. Of those that a mesh axis runs over, the one named last changes fastest.
The devices are a block of a 4x4x8 slice.
Arguments:
- x: bfloat16 [64, 4096, 512], P(('rep', 'dp')), parts along dimension 0
- dy: bfloat16 [64, 4096, 512], P(('rep', 'dp')), parts along dimension 0
- w_gate: bfloat16 [2, 512, 1408], P(None, 'dp')
- w_up: bfloat16 [2, 512, 1408], P(None, 'dp')
- w_down: bfloat16 [2, 1408, 512], P(None, 'dp')
- m_w_gate: float32 [2, 512, 1408], P(None, 'dp')
- m_w_up: float32 [2, 512, 1408], P(None, 'dp')
- m_w_down: float32 [2, 1408, 512], P(None, 'dp')
- v_w_gate: float32 [2, 512, 1408], P(None, 'dp')
- v_w_up: float32 [2, 512, 1408], P(None, 'dp')
- v_w_down: float32 [2, 1408, 512], P(None, 'dp')
Outputs:
- output 1: bfloat16 [8, 512, 1408], P('rep', 'dp'), parts along dimension 0
- output 2: bfloat16 [8, 512, 1408], P('rep', 'dp'), parts along dimension 0
- output 3: bfloat16 [8, 1408, 512], P('rep', 'dp'), parts along dimension 0
- output 4: float32 [8, 512, 1408], P('rep', 'dp'), parts along dimension 0
- output 5: float32 [8, 512, 1408], P('rep', 'dp'), parts along dimension 0
- output 6: float32 [8, 1408, 512], P('rep', 'dp'), parts along dimension 0
- output 7: float32 [8, 512, 1408], P('rep', 'dp'), parts along dimension 0
- output 8: float32 [8, 512, 1408], P('rep', 'dp'), parts along dimension 0
- output 9: float32 [8, 1408, 512], P('rep', 'dp'), parts along dimension 0
There are 4 independent parts. A program takes and returns all parts, laid end to end along the dimension named above; an argument that names none is the same for every part.
All inputs are finite; a program needn't handle non-finite values.
Results may differ from a plain program's by a relative error of at most 0.0225.
Values are sent between devices in bfloat16 or wider.
A program may use at most 768 MiB of HBM per device.

v0:
```python
import jax
import jax.numpy as jnp
from jax import lax
from jax.sharding import PartitionSpec as P

NAMES = ("w_gate", "w_up", "w_down")


def matmul(a, w):
    return jnp.dot(a, w, preferred_element_type=jnp.float32).astype(jnp.bfloat16)


def normed(h):
    wide = h.astype(jnp.float32)
    scale = lax.rsqrt(jnp.mean(wide**2, -1, keepdims=True) + 1e-6)
    return (wide * scale).astype(jnp.bfloat16)


def layer(h, w):
    a = normed(h)
    gate = jnp.dot(a, w["w_gate"], preferred_element_type=jnp.float32)
    up = jnp.dot(a, w["w_up"], preferred_element_type=jnp.float32)
    return h + matmul((jax.nn.silu(gate) * up).astype(jnp.bfloat16), w["w_down"])


def adamw(w, m, v, g):
    m = 0.9 * m + 0.1 * g
    v = 0.95 * v + 0.05 * g * g
    step = m * lax.rsqrt(v + 1e-8) + 0.1 * w
    return (w - 0.02 * step).astype(jnp.bfloat16), m, v


def clipped(gradients, sum_of_squares, count):
    factor = jnp.minimum(1.0, 0.5 * lax.rsqrt(sum_of_squares / count + 1e-30))
    return [g * factor for g in gradients]


def solution(mesh):
    def fetched(weights, number):
        return {name: lax.all_gather(w[number], "dp", axis=0, tiled=True) for name, w in zip(NAMES, weights, strict=True)}

    def step(x, dy, *arrays):
        weights, m, v = (arrays[i : i + 3] for i in (0, 3, 6))
        layers = weights[0].shape[0]
        h, kept = x[0], []
        for number in range(layers):
            kept.append(h)
            h = layer(h, fetched(weights, number))
        by_h, mine = dy[0], [None] * layers
        for number in reversed(range(layers)):
            _, back = jax.vjp(lambda w, h: layer(h, w), fetched(weights, number), kept[number])
            by_w, by_h = back(by_h)
            mine[number] = [lax.psum_scatter(by_w[name], "dp", scatter_dimension=0, tiled=True) for name in NAMES]
        gradients = [jnp.stack([mine[number][i] for number in range(layers)]).astype(jnp.float32) for i in range(3)]
        squares = lax.psum(sum(jnp.sum(g * g) for g in gradients), "dp")
        gradients = clipped(gradients, squares, lax.psum(1, "dp") * sum(g.size for g in gradients))
        new = [adamw(w.astype(jnp.float32), m, v, g) for w, m, v, g in zip(weights, m, v, gradients, strict=True)]
        return tuple(one[which] for which in range(3) for one in new)

    states, cut = P(("rep", "dp"), None, None), P(None, "dp", None)
    return jax.shard_map(
        step,
        mesh=mesh,
        in_specs=(states, states) + (cut,) * 9,
        out_specs=(P("rep", "dp", None),) * 9,
        check_vma=False,
    )
```

profile of v0, /device:TPU:21, one launch (start us, length us, event | category | flops | bytes accessed | tf_op | source)
XLA Modules:
  0.0 670.5 jit_solution(47285392992734594)
XLA Ops:
  7.3 1.6 fusion.93
  8.9 0.1 all-gather.15.cloned.1.call-start
  9.0 1.6 fusion.92
  10.7 0.1 all-gather.17.cloned.1.call-start
  10.8 1.6 fusion.91
  12.5 0.6 all-gather.21.cloned.1.call-update
  13.1 0.6 all-gather.23.cloned.1.call-update
  13.8 0.6 all-gather.19.cloned.1.call-update
  14.4 6.4 copy.20
  20.8 3.1 fusion.15
  23.9 6.3 copy.21
  30.2 20.7 %all-gather.13.cloned.1.call-done = bf16[1,512,1408]{2,1,0:T(8,128)(2,1)} async-done(((bf16[1,32,1408]{2,1,0:T(8,128)(2,1)}), bf16[1,512,1408]{2,1,0:T(8,128)(2,1)}) %all-gather.13.cloned.1.call-update) | async-done | bytes 1441808 | tf_op jit(solution)/shard_map/all_gather | solution.py:40
  50.9 13.2 %fusion.47 = f32[4096,1408]{1,0:T(8,128)} fusion(bf16[1,4096,512]{1,2,0:T(8,128)(2,1)} %copy.20, f32[4096]{0:T(1024)S(1)} %add_rsqrt_fusion, bf16[1,512,1408]{2,1,0:T(8,128)(2,1)} %all-gather.13.cloned.1.call-done), kind=kOutput, calls=%fused_computation.57 | convolution fusion | flops 5911871488 | bytes 28721152 | tf_op jit(solution)/shard_map/dot_general | solution.py:21
  64.1 23.2 %all-gather.15.cloned.1.call-done = bf16[1,512,1408]{2,1,0:T(8,128)(2,1)} async-done(((bf16[1,32,1408]{2,1,0:T(8,128)(2,1)}), bf16[1,512,1408]{2,1,0:T(8,128)(2,1)}) %all-gather.15.cloned.1.call-update) | async-done | bytes 1441808 | tf_op jit(solution)/shard_map/all_gather | solution.py:40
  87.3 24.3 %multiply_convert_fusion.1 = (bf16[4096,1408]{1,0:T(8,128)(2,1)}, f32[4096,1408]{1,0:T(8,128)}) fusion(f32[4096,1408]{1,0:T(8,128)} %fusion.47, bf16[1,512,1408]{2,1,0:T(8,128)(2,1)} %all-gather.15.cloned.1.call-done, bf16[1,4096,512]{1,2,0:T(8,128)(2,1)} %copy.20, f32[4096]{0:T(1024)S(1)} %add_rsqrt_fusion), kind=kOutput, calls=%fused_computation.17 | convolution fusion | flops 5946474496 | bytes 63324160 | tf_op jit(solution)/shard_map/dot_general | solution.py:22
  111.6 12.0 %all-gather.17.cloned.1.call-done = bf16[1,1408,512]{2,1,0:T(8,128)(2,1)} async-done(((bf16[1,88,512]{2,1,0:T(8,128)(2,1)}), bf16[1,1408,512]{2,1,0:T(8,128)(2,1)}) %all-gather.17.cloned.1.call-update) | async-done | bytes 1441808 | tf_op jit(solution)/shard_map/all_gather | solution.py:40
  123.7 12.4 %fusion.19 = (f32[4096]{0:T(1024)S(1)}, bf16[4096,512]{0,1:T(8,128)(2,1)}) fusion(bf16[4096,1408]{1,0:T(8,128)(2,1)} %get-tuple-element.24, bf16[1,1408,512]{2,1,0:T(8,128)(2,1)} %all-gather.17.cloned.1.call-done, bf16[1,4096,512]{1,2,0:T(8,128)(2,1)} %copy.20), kind=kOutput, calls=%fused_computation.37 | convolution fusion | flops 5916061696 | bytes 21381120 | tf_op jit(solution)/shard_map/dot_general | solution.py:10
  136.1 0.6 copy-done.12
  136.7 23.1 %all-gather.21.cloned.1.call-done = bf16[1,1408,512]{2,1,0:T(8,128)(2,1)} async-done(((bf16[1,88,512]{2,1,0:T(8,128)(2,1)}), bf16[1,1408,512]{2,1,0:T(8,128)(2,1)}) %all-gather.21.cloned.1.call-update) | async-done | bytes 1441808 | tf_op jit(solution)/shard_map/all_gather | solution.py:40
  159.9 11.8 %convolution_convert_fusion.1 = bf16[4096,1408]{1,0:T(8,128)(2,1)} fusion(bf16[1,4096,512]{2,1,0:T(8,128)(2,1)} %param.12, bf16[1,1408,512]{2,1,0:T(8,128)(2,1)} %all-gather.21.cloned.1.call-done), kind=kOutput, calls=%fused_computation.23 | convolution fusion | flops 5911347200 | bytes 17170432 | tf_op jit(solution)/shard_map/transpose(jvp())/dot_general | solution.py:10
  171.7 24.4 %all-gather.23.cloned.1.call-done = bf16[1,512,1408]{2,1,0:T(8,128)(2,1)} async-done(((bf16[1,32,1408]{2,1,0:T(8,128)(2,1)}), bf16[1,512,1408]{2,1,0:T(8,128)(2,1)}) %all-gather.23.cloned.1.call-update) | async-done | bytes 1441808 | tf_op jit(solution)/shard_map/all_gather | solution.py:40
  196.1 13.1 %fusion.39 = f32[4096,1408]{1,0:T(8,128)} fusion(bf16[4096,512]{0,1:T(8,128)(2,1)} %get-tuple-element.27, f32[4096]{0:T(1024)S(1)} %fusion.79, bf16[1,512,1408]{2,1,0:T(8,128)(2,1)} %all-gather.23.cloned.1.call-done), kind=kOutput, calls=%fused_computation.54 | convolution fusion | flops 5911871488 | bytes 28721152 | tf_op jit(solution)/shard_map/jvp()/dot_general | solution.py:22
  209.2 23.1 %all-gather.19.cloned.1.call-done = bf16[1,512,1408]{2,1,0:T(8,128)(2,1)} async-done(((bf16[1,32,1408]{2,1,0:T(8,128)(2,1)}), bf16[1,512,1408]{2,1,0:T(8,128)(2,1)}) %all-gather.19.cloned.1.call-update) | async-done | bytes 1441808 | tf_op jit(solution)/shard_map/all_gather | solution.py:40
  232.3 31.8 %fusion.2 = (bf16[4096,1408]{1,0:T(8,128)(2,1)}, f32[4096,1408]{1,0:T(8,128)}) fusion(f32[4096,1408]{1,0:T(8,128)} %fusion.39, bf16[4096,1408]{1,0:T(8,128)(2,1)} %convolution_convert_fusion.1, bf16[1,512,1408]{2,1,0:T(8,128)(2,1)} %all-gather.19.cloned.1.call-done, bf16[4096,512]{0,1:T(8,128)(2,1)} %get-tuple-element.27, f32[4096]{0:T(1024)S(1)} %fusion.79), kind=kOutput, calls=%fused_computation.8 | convolution fusion | flops 5981077504 | bytes 74858496 | tf_op jit(solution)/shard_map/jvp()/dot_general | solution.py:21
  264.1 22.3 %convolution_convert_fusion.5 = bf16[512,1408]{1,0:T(8,128)(2,1)} fusion(bf16[4096,1408]{1,0:T(8,128)(2,1)} %get-tuple-element.28, bf16[4096,512]{0,1:T(8,128)(2,1)} %get-tuple-element.27, f32[4096]{0:T(1024)S(1)} %fusion.79), kind=kOutput, calls=%fused_computation.53 | convolution fusion | flops 5911871488 | bytes 17186816 | tf_op jit(solution)/shard_map/transpose(jvp())/dot_general | solution.py:21
  286.5 0.1 reduce-scatter.7.cloned.1.call-start
  286.6 17.2 %fusion.22 = bf16[4096,512]{0,1:T(8,128)(2,1)} fusion(bf16[4096,1408]{1,0:T(8,128)(2,1)} %convolution_convert_fusion.1, bf16[1,512,1408]{2,1,0:T(8,128)(2,1)} %all-gather.23.cloned.1.call-done, f32[4096,1408]{1,0:T(8,128)} %get-tuple-element.29), kind=kOutput, calls=%fused_computation.40 | convolution fusion | flops 5942280192 | bytes 40239104 | tf_op jit(solution)/shard_map/transpose(jvp())/dot_general | solution.py:22
  303.7 11.1 %fusion.21 = (f32[4096]{0:T(1024)S(1)}, bf16[4096,512]{0,1:T(8,128)(2,1)S(1)}) fusion(bf16[4096,512]{0,1:T(8,128)(2,1)S(1)} %copy-done.1, bf16[4096,512]{0,1:T(8,128)(2,1)} %fusion.22, bf16[4096,1408]{1,0:T(8,128)(2,1)} %get-tuple-element.28, bf16[1,512,1408]{2,1,0:T(8,128)(2,1)} %all-gather.19.cloned.1.call-done), kind=kOutput, calls=%fused_computation.39 | convolution fusion | flops 5916061696 | bytes 25575424 | tf_op jit(solution)/shard_map/transpose(jvp())/dot_general | solution.py:21
  314.9 2.9 fusion.25
  317.8 9.5 %convolution_convert_fusion = bf16[4096,1408]{1,0:T(8,128)(2,1)} fusion(bf16[4096,512]{0,1:T(8,128)(2,1)S(1)} %fusion.25, bf16[1,1408,512]{2,1,0:T(8,128)(2,1)S(1)} %copy-done.16), kind=kOutput, calls=%fused_computation.22 | convolution fusion | flops 5911347200 | bytes 17170432 | tf_op jit(solution)/shard_map/transpose(jvp())/dot_general | solution.py:10
  327.4 24.6 %fusion.33 = bf16[512,1408]{1,0:T(8,128)(2,1)} fusion(f32[4096,1408]{1,0:T(8,128)} %fusion.47, f32[4096,1408]{1,0:T(8,128)} %get-tuple-element.25, bf16[4096,1408]{1,0:T(8,128)(2,1)} %convolution_convert_fusion, bf16[1,4096,512]{1,2,0:T(8,128)(2,1)} %copy.20, f32[4096]{0:T(1024)S(1)} %copy-done.15), kind=kOutput, calls=%fused_computation.50 | convolution fusion | flops 5976031232 | bytes 63324160 | tf_op jit(solution)/shard_map/transpose(jvp())/dot_general | solution.py:21
  352.0 0.1 reduce-scatter.13.cloned.1.call-start
  352.1 17.2 %fusion.32 = bf16[512,1408]{1,0:T(8,128)(2,1)} fusion(bf16[4096,1408]{1,0:T(8,128)(2,1)} %convolution_convert_fusion.1, bf16[4096,512]{0,1:T(8,128)(2,1)} %get-tuple-element.27, f32[4096]{0:T(1024)S(1)} %fusion.79, f32[4096,1408]{1,0:T(8,128)} %get-tuple-element.29), kind=kOutput, calls=%fused_computation.49 | convolution fusion | flops 5947195392 | bytes 40255488 | tf_op jit(solution)/shard_map/transpose(jvp())/dot_general | solution.py:22
  369.4 0.1 reduce-scatter.11.cloned.1.call-start
  369.5 17.6 %fusion.36 = bf16[512,1408]{1,0:T(8,128)(2,1)} fusion(bf16[4096,1408]{1,0:T(8,128)(2,1)} %convolution_convert_fusion, f32[4096,1408]{1,0:T(8,128)} %fusion.47, bf16[1,4096,512]{1,2,0:T(8,128)(2,1)} %copy.20, f32[4096]{0:T(1024)S(1)} %copy-done.15), kind=kOutput, calls=%fused_computation.51 | convolution fusion | flops 5947195392 | bytes 40255488 | tf_op jit(solution)/shard_map/transpose(jvp())/dot_general | solution.py:22
  387.1 0.1 reduce-scatter.17.cloned.1.call-start
  387.2 20.4 %fusion.29 = bf16[1408,512]{1,0:T(8,128)(2,1)} fusion(bf16[1,4096,512]{2,1,0:T(8,128)(2,1)} %param.12, f32[4096,1408]{1,0:T(8,128)} %fusion.39, f32[4096,1408]{1,0:T(8,128)} %get-tuple-element.29), kind=kOutput, calls=%fused_computation.48 | convolution fusion | flops 5940903936 | bytes 51773440 | tf_op jit(solution)/shard_map/transpose(jvp())/dot_general | solution.py:10
  407.9 12.4 %convolution_convert_fusion.4 = bf16[1408,512]{1,0:T(8,128)(2,1)} fusion(bf16[4096,1408]{1,0:T(8,128)(2,1)} %get-tuple-element.24, bf16[4096,512]{0,1:T(8,128)(2,1)} %copy-done.2), kind=kOutput, calls=%fused_computation.52 | convolution fusion | flops 5906300928 | bytes 17170432 | tf_op jit(solution)/shard_map/transpose(jvp())/dot_general | solution.py:10
  420.4 1.6 fusion.67
  422.0 37.4 %reduce-scatter.13.cloned.1.call-done = bf16[32,1408]{1,0:T(8,128)(2,1)} async-done(((bf16[512,1408]{1,0:T(8,128)(2,1)}), bf16[32,1408]{1,0:T(8,128)(2,1)}) %reduce-scatter.13.cloned.1.call-update) | async-done | bytes 90128 | tf_op jit(solution)/shard_map/reduce_scatter | solution.py:53
  459.4 56.5 %reduce-scatter.11.cloned.1.call-done = bf16[32,1408]{1,0:T(8,128)(2,1)} async-done(((bf16[512,1408]{1,0:T(8,128)(2,1)}), bf16[32,1408]{1,0:T(8,128)(2,1)}) %reduce-scatter.11.cloned.1.call-update) | async-done | bytes 90128 | tf_op jit(solution)/shard_map/reduce_scatter | solution.py:53
  515.9 1.6 fusion.68
  518.8 53.7 %reduce-scatter.17.cloned.1.call-done = bf16[88,512]{1,0:T(8,128)(2,1)} async-done(((bf16[1408,512]{1,0:T(8,128)(2,1)}), bf16[88,512]{1,0:T(8,128)(2,1)}) %reduce-scatter.17.cloned.1.call-update) | async-done | bytes 90128 | tf_op jit(solution)/shard_map/reduce_scatter | solution.py:53
  572.5 56.5 %reduce-scatter.15.cloned.1.call-done = bf16[88,512]{1,0:T(8,128)(2,1)} async-done(((bf16[1408,512]{1,0:T(8,128)(2,1)}), bf16[88,512]{1,0:T(8,128)(2,1)}) %reduce-scatter.15.cloned.1.call-update) | async-done | bytes 90128 | tf_op jit(solution)/shard_map/reduce_scatter | solution.py:53
  629.0 1.6 fusion.69
  631.3 27.0 %psum.7 = f32[]{:T(128)} all-reduce(f32[]{:T(128)S(6)} %add.99), channel_id=1, replica_groups=mesh['rep'=4,'dp'=16] {'dp'}, use_global_device_ids=true, to_apply=%region_12.13 | all-reduce | flops 1 | bytes 8 | tf_op jit(solution)/shard_map/psum | solution.py:55
  659.1 1.9 fusion.75
  661.0 2.4 fusion.66
  (53 shorter events, 1.0 us)
Async XLA Ops:
  7.2 43.8 %all-gather.13.cloned.1.call-start = ((), (), s32[]{:S(2)}) async-start(), calls=%async_computation.12 | async-start | bytes 1531904 | tf_op jit(solution)/shard_map/all_gather | solution.py:40
  8.9 78.4 %all-gather.15.cloned.1.call-start = ((), (), s32[]{:S(2)}) async-start(), calls=%async_computation.13 | async-start | bytes 1531904 | tf_op jit(solution)/shard_map/all_gather | solution.py:40
  10.7 113.0 %all-gather.17.cloned.1.call-start = ((), (), s32[]{:S(2)}) async-start(), calls=%async_computation.14 | async-start | bytes 1531904 | tf_op jit(solution)/shard_map/all_gather | solution.py:40
  12.4 147.4 %all-gather.21.cloned.1.call-start = ((), (), s32[]{:S(2)}) async-start(), calls=%async_computation.16 | async-start | bytes 1531904 | tf_op jit(solution)/shard_map/all_gather | solution.py:40
  13.1 183.0 %all-gather.23.cloned.1.call-start = ((), (), s32[]{:S(2)}) async-start(), calls=%async_computation.17 | async-start | bytes 1531904 | tf_op jit(solution)/shard_map/all_gather | solution.py:40
  13.7 218.6 %all-gather.19.cloned.1.call-start = ((), (), s32[]{:S(2)}) async-start(), calls=%async_computation.15 | async-start | bytes 1531904 | tf_op jit(solution)/shard_map/all_gather | solution.py:40
  14.4 406.0 %reduce-scatter.9.cloned.1.call-start = ((), (), s32[]{:S(2)}) async-start(), calls=%async_computation.7 | async-start | bytes 1531904 | tf_op jit(solution)/shard_map/reduce_scatter | solution.py:53
  23.9 63.4 %copy-start.14 = (f32[4096]{0:T(1024)}, f32[4096]{0:T(1024)S(1)}, u32[]{:S(2)}) copy-start(f32[4096]{0:T(1024)S(1)} %add_rsqrt_fusion) | copy-start | bytes 49156
  136.1 0.6 copy-start.12
  286.5 133.9 %reduce-scatter.7.cloned.1.call-start = ((), (), s32[]{:S(2)}) async-start(), calls=%async_computation.6 | async-start | bytes 1531904 | tf_op jit(solution)/shard_map/reduce_scatter | solution.py:53
  286.5 17.2 %copy-start.1 = (bf16[4096,512]{0,1:T(8,128)(2,1)S(1)}, bf16[4096,512]{0,1:T(8,128)(2,1)}, u32[]{:S(2)}) copy-start(bf16[4096,512]{0,1:T(8,128)(2,1)} %get-tuple-element.27) | copy-start | bytes 12582916
  303.7 11.2 %copy-start.13 = (f32[4096]{0:T(1024)S(1)}, f32[4096]{0:T(1024)}, u32[]{:S(2)}) copy-start(f32[4096]{0:T(1024)} %copy-done.12) | copy-start | bytes 49156
  303.7 11.2 %copy-start = (bf16[1,4096,512]{1,2,0:T(8,128)(2,1)S(1)}, bf16[1,4096,512]{1,2,0:T(8,128)(2,1)}, u32[]{:S(2)}) copy-start(bf16[1,4096,512]{1,2,0:T(8,128)(2,1)} %copy.21) | copy-start | bytes 12582916
  314.9 2.9 copy-start.16
  317.8 9.6 %copy-start.2 = (bf16[4096,512]{0,1:T(8,128)(2,1)}, bf16[4096,512]{0,1:T(8,128)(2,1)S(1)}, u32[]{:S(2)}) copy-start(bf16[4096,512]{0,1:T(8,128)(2,1)S(1)} %fusion.25) | copy-start | bytes 12582916
  317.8 9.5 %copy-start.15 = (f32[4096]{0:T(1024)S(1)}, f32[4096]{0:T(1024)}, u32[]{:S(2)}) copy-start(f32[4096]{0:T(1024)} %copy-done.14) | copy-start | bytes 49156
  352.0 107.4 %reduce-scatter.13.cloned.1.call-start = ((), (), s32[]{:S(2)}) async-start(), calls=%async_computation.9 | async-start | bytes 1531904 | tf_op jit(solution)/shard_map/reduce_scatter | solution.py:53
  369.4 146.5 %reduce-scatter.11.cloned.1.call-start = ((), (), s32[]{:S(2)}) async-start(), calls=%async_computation.8 | async-start | bytes 1531904 | tf_op jit(solution)/shard_map/reduce_scatter | solution.py:53
  387.1 185.4 %reduce-scatter.17.cloned.1.call-start = ((), (), s32[]{:S(2)}) async-start(), calls=%async_computation.11 | async-start | bytes 1531904 | tf_op jit(solution)/shard_map/reduce_scatter | solution.py:53
  407.7 251.4 %copy-start.5 = (bf16[2,88,512]{2,1,0:T(8,128)(2,1)S(1)}, bf16[2,88,512]{2,1,0:T(8,128)(2,1)}, u32[]{:S(2)}) copy-start(bf16[2,88,512]{2,1,0:T(8,128)(2,1)} %param.15) | copy-start | bytes 540676
  407.7 251.4 %copy-start.6 = (f32[2,88,512]{2,1,0:T(8,128)S(1)}, f32[2,88,512]{2,1,0:T(8,128)}, u32[]{:S(2)}) copy-start(f32[2,88,512]{2,1,0:T(8,128)} %param.21) | copy-start | bytes 1081348
  407.7 251.4 %copy-start.7 = (f32[2,88,512]{2,1,0:T(8,128)S(1)}, f32[2,88,512]{2,1,0:T(8,128)}, u32[]{:S(2)}) copy-start(f32[2,88,512]{2,1,0:T(8,128)} %param.18) | copy-start | bytes 1081348
  407.7 253.3 %copy-start.3 = (bf16[2,32,1408]{2,1,0:T(8,128)(2,1)S(1)}, bf16[2,32,1408]{2,1,0:T(8,128)(2,1)}, u32[]{:S(2)}) copy-start(bf16[2,32,1408]{2,1,0:T(8,128)(2,1)} %param.13) | copy-start | bytes 540676
  407.7 253.3 %copy-start.4 = (bf16[2,32,1408]{2,1,0:T(8,128)(2,1)S(1)}, bf16[2,32,1408]{2,1,0:T(8,128)(2,1)}, u32[]{:S(2)}) copy-start(bf16[2,32,1408]{2,1,0:T(8,128)(2,1)} %param.14) | copy-start | bytes 540676
  407.7 253.3 %copy-start.8 = (f32[2,32,1408]{2,1,0:T(8,128)S(1)}, f32[2,32,1408]{2,1,0:T(8,128)}, u32[]{:S(2)}) copy-start(f32[2,32,1408]{2,1,0:T(8,128)} %param.19) | copy-start | bytes 1081348
  407.7 253.3 %copy-start.9 = (f32[2,32,1408]{2,1,0:T(8,128)S(1)}, f32[2,32,1408]{2,1,0:T(8,128)}, u32[]{:S(2)}) copy-start(f32[2,32,1408]{2,1,0:T(8,128)} %param.16) | copy-start | bytes 1081348
  407.8 253.3 %copy-start.10 = (f32[2,32,1408]{2,1,0:T(8,128)S(1)}, f32[2,32,1408]{2,1,0:T(8,128)}, u32[]{:S(2)}) copy-start(f32[2,32,1408]{2,1,0:T(8,128)} %param.20) | copy-start | bytes 1081348
  407.8 253.3 %copy-start.11 = (f32[2,32,1408]{2,1,0:T(8,128)S(1)}, f32[2,32,1408]{2,1,0:T(8,128)}, u32[]{:S(2)}) copy-start(f32[2,32,1408]{2,1,0:T(8,128)} %param.17) | copy-start | bytes 1081348
  407.8 221.2 %reduce-scatter.15.cloned.1.call-start = ((), (), s32[]{:S(2)}) async-start(), calls=%async_computation.10 | async-start | bytes 1531904 | tf_op jit(solution)/shard_map/reduce_scatter | solution.py:53
Sparse Core Ops, SparseCore 0:
  10.2 40.6 all-gather.12
  53.1 34.1 all-gather.14
  89.5 34.1 all-gather.16
  125.7 34.0 all-gather.20
  161.9 34.1 all-gather.22
  198.1 34.1 all-gather.18
  286.6 50.8 reduce-scatter.8
  352.1 50.6 reduce-scatter.6
  405.1 54.2 reduce-scatter.12
  461.6 54.2 reduce-scatter.10
  518.2 54.2 reduce-scatter.16
  574.7 54.2 reduce-scatter.14
where the time goes:
time: 680 us; the launch traced here: 670 us
  waiting for transfers between devices  333 us (49%)
  matrix products  259 us (38%)
  blocking collectives  27 us (4%)
  local copies, waits for them, and re-layouts  18.2 us (3%)
  between operations  17.3 us (3%)
  other arithmetic  15.2 us (2%)
    reduce_scatter x6, waiting for transfers between devices, step(): lax.psum_scatter(by_w[name], 'dp', scatter_dimension=0, tiled=True)  204 us
    all_gather x6, waiting for transfers between devices, fetched(): lax.all_gather(w[number], 'dp', axis=0, tiled=True)  127 us
    dot_general x5, matrix products, layer(): gate = jnp.dot(a, w['w_gate'], preferred_element_type=jnp.float32)  103 us
    dot_general x5, matrix products, layer(): up = jnp.dot(a, w['w_up'], preferred_element_type=jnp.float32)  89.4 us
    dot_general x5, matrix products, matmul(): jnp.dot(a, w, preferred_element_type=jnp.float32).astype(jnp.bfloat16)  66.6 us
    psum x1, blocking collectives, step(): squares = lax.psum(sum((jnp.sum(g * g) for g in gradients)), 'dp')  27 us
  transfers between devices with their start and end apart: 12, of which 10 were waited for; matrix products, arithmetic and copies ran while one was open for 34% of the time, Pallas kernels for 0%

commit v1 on v0

v1 whole, which is shorter than its diff:
```python
import functools

import jax
import jax.numpy as jnp
from jax import lax
from jax.experimental import pallas as pl
from jax.experimental.pallas import tpu as pltpu
from jax.sharding import PartitionSpec as P

F32, BF16 = jnp.float32, jnp.bfloat16
TILE = 512
VMEM_LIMIT = 60 << 20
MESH = pl.DeviceIdType.MESH


def dot(a, b):
    return jnp.dot(a, b, preferred_element_type=F32)


def norm_parts(h):
    wide = h.astype(F32)
    scale = lax.rsqrt(jnp.mean(wide * wide, -1, keepdims=True) + 1e-6)
    return wide, scale, (wide * scale).astype(BF16)


def sigmoid(x):
    return 0.5 * jnp.tanh(0.5 * x) + 0.5


class Place:
    def __init__(self, chips):
        me = lax.axis_index("dp")
        self.chips, self.half = chips, chips // 2
        self.z, self.c = me // 2, me % 2
        self.sibling = self.z * 2 + 1 - self.c

    def chip(self, offset):
        return lax.rem(self.z + offset + 2 * self.chips, self.chips)

    def beside(self, direction):
        return self.chip(direction) * 2 + self.c


def meet(devices):
    barrier = pltpu.get_barrier_semaphore()
    for device in devices:
        pl.semaphore_signal(barrier, inc=1, device_id={"dp": device}, device_id_type=MESH)
    pl.semaphore_wait(barrier, len(devices))


def remote(src, dst, send, recv, device):
    return pltpu.make_async_remote_copy(src_ref=src, dst_ref=dst, send_sem=send, recv_sem=recv, device_id={"dp": device}, device_id_type=MESH)


DIRECTIONS = (1, -1)


class Gather:
    def __init__(self, place, shards, fulls, signs, ring_send, ring_recv, side_send, side_recv, own_sem):
        self.p, self.shards, self.fulls, self.signs = place, shards, fulls, signs
        self.sems = (ring_send, ring_recv, side_send, side_recv, own_sem)

    @staticmethod
    def scratch(chips, matrices):
        ring, side = 2 * (chips // 2) * matrices, (2 * (chips // 2) + 1) * matrices
        dma = pltpu.SemaphoreType.DMA
        return [dma((ring,)), dma((ring,)), dma((side,)), dma((side,)), dma((matrices,))]

    def goes(self, direction, step, m):
        return step < self.p.half - 1 or self.signs[m] == direction

    def ring(self, direction, step, m):
        p, k = self.p, ((direction < 0) * self.p.half + step) * len(self.fulls) + m
        place = self.fulls[m].at[p.chip(-direction * step), p.c]
        return remote(self.shards[m] if step == 0 else place, place, self.sems[0].at[k], self.sems[1].at[k], p.beside(direction))

    def side(self, direction, step, m):
        p, n = self.p, len(self.fulls)
        k = (0 if step == 0 else 1 + (direction < 0) * p.half + step - 1) * n + m
        place = self.fulls[m].at[p.chip(-direction * step), p.c]
        return remote(self.shards[m] if step == 0 else place, place, self.sems[2].at[k], self.sems[3].at[k], p.sibling)

    def own(self, m):
        return pltpu.make_async_copy(self.shards[m], self.fulls[m].at[self.p.z, self.p.c], self.sems[4].at[m])

    def step(self, step):
        matrices = range(len(self.fulls))
        for m in matrices:
            for direction in DIRECTIONS:
                if step > 0 and self.goes(direction, step - 1, m):
                    self.ring(direction, step - 1, m).wait_recv()
                if step < self.p.half and self.goes(direction, step, m):
                    self.ring(direction, step, m).start()
                if step > 0 and self.goes(direction, step - 1, m):
                    self.side(direction, step, m).start()
            if step == 0:
                self.side(1, 0, m).start()
                self.own(m).start()

    def finish(self):
        for m in range(len(self.fulls)):
            self.own(m).wait()
            self.side(1, 0, m).wait()
            for direction in DIRECTIONS:
                for step in range(self.p.half):
                    if self.goes(direction, step, m):
                        self.ring(direction, step, m).wait_send()
                        self.side(direction, step + 1, m).wait()


class Scatter:
    def __init__(self, place, terms, signs, scratch):
        self.p, self.terms, self.signs, n = place, terms, signs, len(terms)
        self.own, self.other, self.sent, self.came = (scratch[i * n : (i + 1) * n] for i in range(4))
        self.own_sem, self.pair_send, self.pair_recv, self.ring_send, self.ring_recv = scratch[4 * n :]

    @staticmethod
    def scratch(chips, shapes):
        steps, n, dma = chips // 2, len(shapes), pltpu.SemaphoreType.DMA
        blocks = [pltpu.VMEM((chips, *shape), BF16) for shape in shapes]
        slots = [pltpu.VMEM((2 * steps, *shape), BF16) for shape in shapes]
        return blocks * 2 + slots * 2 + [dma((n,)), dma((n,)), dma((n,)), dma((2 * steps * n,)), dma((2 * steps * n,))]

    def local(self, m):
        return pltpu.make_async_copy(self.terms[m].at[:, self.p.c], self.own[m], self.own_sem.at[m])

    def pair(self, m):
        return remote(self.terms[m].at[:, 1 - self.p.c], self.other[m], self.pair_send.at[m], self.pair_recv.at[m], self.p.sibling)

    def goes(self, direction, step, m):
        return step > 0 or self.signs[m] == direction

    def slot(self, direction, step):
        return (direction < 0) * self.p.half + step

    def ring(self, direction, step, m):
        slot = self.slot(direction, step)
        k = slot * len(self.terms) + m
        return remote(self.sent[m].at[slot], self.came[m].at[slot], self.ring_send.at[k], self.ring_recv.at[k], self.p.beside(direction))

    def exchange(self):
        for m in range(len(self.terms)):
            self.pair(m).start()
            self.local(m).start()

    def mine(self, m, t):
        return self.own[m][t].astype(F32) + self.other[m][t].astype(F32)

    def step(self, step):
        for m in range(len(self.terms)):
            if step == 0:
                self.local(m).wait()
                self.pair(m).wait_recv()
            for direction in DIRECTIONS:
                if not self.goes(direction, step, m):
                    continue
                value = self.mine(m, self.p.chip(direction * (self.p.half - step)))
                if step > 0 and self.goes(direction, step - 1, m):
                    self.ring(direction, step - 1, m).wait_recv()
                    value = value + self.came[m][self.slot(direction, step - 1)].astype(F32)
                self.sent[m][self.slot(direction, step)] = value.astype(BF16)
                self.ring(direction, step, m).start()

    def result(self, m):
        last = self.p.half - 1
        value = self.mine(m, self.p.z)
        for direction in DIRECTIONS:
            self.ring(direction, last, m).wait_recv()
            value = value + self.came[m][self.slot(direction, last)].astype(F32)
        return value.astype(BF16)

    def finish(self):
        for m in range(len(self.terms)):
            self.pair(m).wait_send()
            for direction in DIRECTIONS:
                for step in range(self.p.half):
                    if self.goes(direction, step, m):
                        self.ring(direction, step, m).wait_send()


GATHER_SIGNS = (1, -1, 1)


def gather_kernel(chips, *refs):
    shards, fulls, sems = refs[:3], refs[3:6], refs[6:]
    place = Place(chips)
    meet([place.sibling, place.beside(1), place.beside(-1)])
    gather = Gather(place, shards, fulls, GATHER_SIGNS, *sems)
    for step in range(place.half + 1):
        gather.step(step)
    gather.finish()


def forward_kernel(chips, x, wg, wu, wd, s0, s1, s2, h_out, act_out, f0, f1, f2, *sems):
    i, n = pl.program_id(0), pl.num_programs(0)
    place = Place(chips)
    gather = Gather(place, (s0, s1, s2), (f0, f1, f2), GATHER_SIGNS, *sems)
    for step in range(place.half + 1):

        @pl.when(i == (3 * step) // 2)
        def _(step=step):
            if step == 0:
                meet([place.sibling, place.beside(1), place.beside(-1)])
            gather.step(step)

    h = x[...]
    _, _, a = norm_parts(h)
    gate, up = dot(a, wg[...]), dot(a, wu[...])
    act = (gate * sigmoid(gate) * up).astype(BF16)
    act_out[...] = act
    out = dot(act, wd[...]).astype(BF16)
    h_out[...] = (h.astype(F32) + out.astype(F32)).astype(BF16)

    @pl.when(i == n - 1)
    def _():
        gather.finish()


def backward_act(a, by_out, wg, wu, wdt):
    gate, up = dot(a, wg), dot(a, wu)
    by_act = dot(by_out, wdt).astype(BF16).astype(F32)
    sig = sigmoid(gate)
    silu = gate * sig
    act = (silu * up).astype(BF16)
    by_up = (by_act * silu).astype(BF16)
    by_gate = (by_act * up * (sig + silu * (1.0 - sig))).astype(BF16)
    return act, by_gate, by_up


def both_kernel(h, dy, act0, wg, wu, wd, dh_out, gg, gu, gd, gd0, wgt, wut, wdt, ag, au, ad, ad0):
    i, n = pl.program_id(0), pl.num_programs(0)

    @pl.when(i == 0)
    def _():
        wgt[...] = wg[...].T
        wut[...] = wu[...].T
        wdt[...] = wd[...].T
        for acc in (ag, au, ad, ad0):
            acc[...] = jnp.zeros_like(acc)

    by_out = dy[...]
    wide, scale, a = norm_parts(h[...])
    act, by_gate, by_up = backward_act(a, by_out, wg[...], wu[...], wdt[...])
    at = a.T
    ag[...] += dot(at, by_gate)
    au[...] += dot(at, by_up)
    ad[...] += dot(by_out.T, act)
    by_a = dot(by_gate, wgt[...]).astype(BF16).astype(F32) + dot(by_up, wut[...]).astype(BF16).astype(F32)
    by_a = by_a.astype(BF16).astype(F32)
    by_wide = by_a * scale - wide * (scale * scale * scale * jnp.mean(by_a * wide, -1, keepdims=True))
    by_h = (by_out.astype(F32) + by_wide.astype(BF16).astype(F32)).astype(BF16)
    dh_out[...] = by_h
    ad0[...] += dot(by_h.T, act0[...])

    @pl.when(i == n - 1)
    def _():
        gg[...] = ag[...].astype(BF16)
        gu[...] = au[...].astype(BF16)
        gd[...] = ad[...].astype(BF16).T
        gd0[...] = ad0[...].astype(BF16).T


def backward_kernel(chips, x, dh, wg, wu, wd, t0, t1, t2, t3, gg, gu, r0, r1, r2, r3, wdt, ag, au, *scratch):
    i, n = pl.program_id(0), pl.num_programs(0)
    place = Place(chips)
    scatter = Scatter(place, (t0, t1, t2, t3), (1, -1, 1, -1), scratch)

    @pl.when(i == 0)
    def _():
        meet([place.sibling, place.beside(1), place.beside(-1)])
        scatter.exchange()
        wdt[...] = wd[...].T
        ag[...] = jnp.zeros_like(ag)
        au[...] = jnp.zeros_like(au)

    for step in range(place.half):

        @pl.when(i == step + 1)
        def _(step=step):
            scatter.step(step)

    _, _, a = norm_parts(x[...])
    _, by_gate, by_up = backward_act(a, dh[...], wg[...], wu[...], wdt[...])
    at = a.T
    ag[...] += dot(at, by_gate)
    au[...] += dot(at, by_up)

    @pl.when(i == n - 1)
    def _():
        for m, out in enumerate((r0, r1, r2, r3)):
            out[...] = scatter.result(m)
        scatter.finish()
        gg[...] = ag[...].astype(BF16)
        gu[...] = au[...].astype(BF16)


def last_kernel(chips, t0, t1, g0, g1, g2, g3, r0, r1, total, part, parts, part_send, part_recv, *scratch):
    place = Place(chips)
    n = 2 * chips
    me = lax.axis_index("dp")
    scatter = Scatter(place, (t0, t1), (1, -1), scratch)
    meet([lax.rem(me + k, n) for k in range(1, n)])
    scatter.exchange()
    squares = jnp.zeros((8, 128), F32)

    def add_up(squares, g):
        g = g.astype(F32)
        g = (g * g).reshape(g.shape[0] // 8, 8, g.shape[1]).sum(0)
        return squares + sum(g[:, k : k + 128] for k in range(0, g.shape[1], 128))

    for g in (g0, g1, g2, g3):
        squares = add_up(squares, g[...])
    for step in range(place.half):
        scatter.step(step)
    for m, out in enumerate((r0, r1)):
        value = scatter.result(m)
        out[...] = value
        squares = add_up(squares, value)
    part[...] = squares
    copies = [remote(part, parts.at[n - k - 1], part_send.at[k - 1], part_recv.at[n - k - 1], lax.rem(me + k, n)) for k in range(1, n)]
    for copy in copies:
        copy.start()
    total_squares = squares
    for k in range(1, n):
        remote(part, parts.at[k - 1], part_send.at[k - 1], part_recv.at[k - 1], lax.rem(me + k, n)).wait_recv()
        total_squares = total_squares + parts[k - 1]
    for copy in copies:
        copy.wait_send()
    scatter.finish()
    total[...] = total_squares


def whole(shape=None):
    return pl.BlockSpec(memory_space=pltpu.VMEM) if shape is None else pl.BlockSpec(shape, lambda i: (0,) * len(shape), pipeline_mode=pl.Buffered(1))


def params(collective=None, **more):
    if collective is not None:
        more.update(collective_id=collective, has_side_effects=True)
    return pltpu.CompilerParams(vmem_limit_bytes=VMEM_LIMIT, **more)


def adamw(w, m, v, g):
    m = 0.9 * m + 0.1 * g
    v = 0.95 * v + 0.05 * g * g
    step = m * lax.rsqrt(v + 1e-8) + 0.1 * w
    return (w - 0.02 * step).astype(BF16), m, v


def solution(mesh):
    group = mesh.shape["dp"]
    chips = group // 2
    any_space = pl.BlockSpec(memory_space=pl.ANY)

    def step(x, dy, *arrays):
        weights, ms, vs = (arrays[i : i + 3] for i in (0, 3, 6))
        x, dy = x[0], dy[0]
        tokens, d = x.shape
        tiles = tokens // TILE
        rows = [(w.shape[1], w.shape[2]) for w in weights]
        ff = rows[0][1]
        shards = [[w[layer] for w in weights] for layer in range(2)]
        full_types = [jax.ShapeDtypeStruct((chips, 2, *r), BF16) for r in rows]
        joined = [(group * r[0], r[1]) for r in rows]

        def join(fulls):
            return [f.reshape(j) for f, j in zip(fulls, joined)]

        def split(g, m):
            return g.reshape(chips, 2, *rows[m])

        w0 = pl.pallas_call(
            functools.partial(gather_kernel, chips),
            out_shape=full_types,
            in_specs=[whole()] * 3,
            out_specs=[whole()] * 3,
            scratch_shapes=Gather.scratch(chips, 3),
            compiler_params=params(0),
            name="gather0",
        )(*shards[0])
        w0 = join(w0)

        narrow = pl.BlockSpec((TILE, d), lambda i: (i, 0))
        broad = pl.BlockSpec((TILE, ff), lambda i: (i, 0))
        weight_specs = [whole(j) for j in joined]
        tokens_d = jax.ShapeDtypeStruct((tokens, d), BF16)
        tokens_ff = jax.ShapeDtypeStruct((tokens, ff), BF16)
        h1, act0, *w1 = pl.pallas_call(
            functools.partial(forward_kernel, chips),
            grid=(tiles,),
            out_shape=[tokens_d, tokens_ff, *full_types],
            in_specs=[narrow, *weight_specs, *[whole(r) for r in rows]],
            out_specs=[narrow, broad, *[any_space] * 3],
            scratch_shapes=Gather.scratch(chips, 3),
            compiler_params=params(1, dimension_semantics=("arbitrary",)),
            name="forward0",
        )(x, *w0, *shards[1])
        w1 = join(w1)

        wide = jax.ShapeDtypeStruct((d, ff), BF16)
        tall = jax.ShapeDtypeStruct((ff, d), BF16)
        dh, gg1, gu1, gd1, gd0 = pl.pallas_call(
            both_kernel,
            grid=(tiles,),
            out_shape=[tokens_d, wide, wide, tall, tall],
            in_specs=[narrow, narrow, broad, *weight_specs],
            out_specs=[narrow, whole((d, ff)), whole((d, ff)), whole((ff, d)), whole((ff, d))],
            scratch_shapes=[pltpu.VMEM((ff, d), BF16), pltpu.VMEM((ff, d), BF16), pltpu.VMEM((d, ff), BF16)] + [pltpu.VMEM((d, ff), F32)] * 4,
            compiler_params=params(dimension_semantics=("arbitrary",)),
            name="both1",
        )(h1, dy, act0, *w1)

        blocks = [jax.ShapeDtypeStruct(r, BF16) for r in rows]
        gg0, gu0, rg1, ru1, rd1, rd0 = pl.pallas_call(
            functools.partial(backward_kernel, chips),
            grid=(tiles,),
            out_shape=[wide, wide, *blocks, blocks[2]],
            in_specs=[narrow, narrow, *weight_specs, *[any_space] * 4],
            out_specs=[whole((d, ff)), whole((d, ff)), *[whole(r) for r in rows], whole(rows[2])],
            scratch_shapes=[pltpu.VMEM((d, ff), BF16)] + [pltpu.VMEM((d, ff), F32)] * 2 + Scatter.scratch(chips, [*rows, rows[2]]),
            compiler_params=params(2, dimension_semantics=("arbitrary",)),
            name="backward0",
        )(x, dh, *w0, split(gg1, 0), split(gu1, 1), split(gd1, 2), split(gd0, 2))

        rg0, ru0, total = pl.pallas_call(
            functools.partial(last_kernel, chips),
            out_shape=[blocks[0], blocks[1], jax.ShapeDtypeStruct((8, 128), F32)],
            in_specs=[any_space] * 2 + [whole()] * 4,
            out_specs=[whole()] * 3,
            scratch_shapes=[pltpu.VMEM((8, 128), F32), pltpu.VMEM((group - 1, 8, 128), F32)]
            + [pltpu.SemaphoreType.DMA((group - 1,))] * 2
            + Scatter.scratch(chips, rows[:2]),
            compiler_params=params(3),
            name="scatter0",
        )(split(gg0, 0), split(gu0, 1), rg1, ru1, rd1, rd0)

        count = group * sum(w.size for w in weights)
        factor = jnp.minimum(1.0, 0.5 * lax.rsqrt(jnp.sum(total) / count + 1e-30))
        gradients = [jnp.stack(pair).astype(F32) * factor for pair in ((rg0, rg1), (ru0, ru1), (rd0, rd1))]
        new = [adamw(w.astype(F32), m, v, g) for w, m, v, g in zip(weights, ms, vs, gradients, strict=True)]
        return tuple(one[which] for which in range(3) for one in new)

    states, cut = P(("rep", "dp"), None, None), P(None, "dp", None)
    return jax.shard_map(
        step,
        mesh=mesh,
        in_specs=(states, states) + (cut,) * 9,
        out_specs=(P("rep", "dp", None),) * 9,
        check_vma=False,
    )
```

time: 680 us -> 253 us (0.37); the launches traced: 670 us -> 253 us
  waiting for transfers between devices: 333 us -> 0 us
  matrix products: 259 us -> 0 us
  Pallas kernels: 0 us -> 242 us
  blocking collectives: 27 us -> 0 us
  between operations: 17.3 us -> 1.53 us
  local copies, waits for them, and re-layouts: 18.2 us -> 3.9 us
  other arithmetic: 15.2 us -> 5.3 us
    dot_general x15 -> x0, matrix products: 259 us -> none  [the longest x5 103 us: layer(): gate = jnp.dot(a, w['w_gate'], preferred_element_type=jnp.float32)]
    pallas_call x0 -> x5, Pallas kernels: none -> 242 us  [the longest x1 77.4 us: step(): pl.pallas_call(both_kernel, grid=(tiles,), out_shape=[tokens_d, wide, wid...]
    reduce_scatter x6 -> x0, waiting for transfers between devices: 204 us -> none  [step(): lax.psum_scatter(by_w[name], 'dp', scatter_dimension=0, tiled=True)]
    all_gather x6 -> x0, waiting for transfers between devices: 127 us -> none  [fetched(): lax.all_gather(w[number], 'dp', axis=0, tiled=True)]
    psum x1 -> x0, blocking collectives: 27 us -> none  [step(): squares = lax.psum(sum((jnp.sum(g * g) for g in gradients)), 'dp')]
    unnamed x36 -> x28, local copies, waits for them, and re-layouts: 13.4 us -> 0.53 us
  transfers between devices with their start and end apart: 12 -> 0, of which waited for: 10 -> 0; matrix products, arithmetic and copies ran while one was open for 34% -> 0% of each run, Pallas kernels for 0% -> 0%
where the time goes in v1:
time: 253 us
  Pallas kernels  242 us (96%)
  other arithmetic  5.3 us (2%)
  local copies, waits for them, and re-layouts  3.9 us (2%)
    pallas_call x1, Pallas kernels, step(): pl.pallas_call(both_kernel, grid=(tiles,), out_shape=[tokens_d, wide, wid...  77.4 us
    pallas_call x1, Pallas kernels, step(): pl.pallas_call(functools.partial(backward_kernel, chips), grid=(tiles,),...  56.4 us
    pallas_call x1, Pallas kernels, step(): pl.pallas_call(functools.partial(forward_kernel, chips), grid=(tiles,), o...  37.2 us
    pallas_call x1, Pallas kernels, step(): pl.pallas_call(functools.partial(gather_kernel, chips), out_shape=full_ty...  36.9 us
    pallas_call x1, Pallas kernels, step(): pl.pallas_call(functools.partial(last_kernel, chips), out_shape=[blocks[0...  34 us

profile of v1, /device:TPU:21, one launch (start us, length us, event | category | flops | bytes accessed | tf_op | source)
XLA Modules:
  0.0 252.6 jit_solution(9658053742218903106)
XLA Ops:
  0.6 1.6 slice_bitcast_fusion
  2.3 1.8 slice_bitcast_fusion.1
  4.0 36.9 %gather0.1 = (bf16[8,2,32,1408]{3,2,1,0:T(8,128)(2,1)}, bf16[8,2,32,1408]{3,2,1,0:T(8,128)(2,1)}, bf16[8,2,88,512]{3,2,1,0:T(8,128)(2,1)}) custom-call(bf16[32,1408]{1,0:T(8,128)(2,1)} %get-tuple-element.68.refs_0_, bf16[32,1408]{1,0:T(8,128)(2,1)} %get-tuple-element.65.refs_1_, bf16[88,512]{1,0:T(8,128)(2,1)} %get-tuple-element.63.refs_2_), custom_call_target="tpu_custom_call" | custom-call | tf_op jit(solution)/shard_map/gather0/pallas_call | solution.py:372
  40.9 37.2 %forward0.1 = (bf16[4096,512]{1,0:T(8,128)(2,1)}, bf16[4096,1408]{1,0:T(8,128)(2,1)}, bf16[8,2,32,1408]{3,2,1,0:T(8,128)(2,1)}, bf16[8,2,32,1408]{3,2,1,0:T(8,128)(2,1)}, bf16[8,2,88,512]{3,2,1,0:T(8,128)(2,1)}) custom-call(bf16[4096,512]{1,0:T(8,128)(2,1)} %bitcast.32, bf16[512,1408]{1,0:T(8,128)(2,1)} %bitcast.34, bf16[512,1408]{1,0:T(8,128)(2,1)} %bitcast.36, ...), custom_call_target="tpu_custom_call" | custom-call | tf_op jit(solution)/shard_map/forward0/pallas_call | solution.py:388
  78.1 77.4 %both1.1 = (bf16[4096,512]{1,0:T(8,128)(2,1)}, bf16[512,1408]{1,0:T(8,128)(2,1)}, bf16[512,1408]{1,0:T(8,128)(2,1)}, bf16[1408,512]{1,0:T(8,128)(2,1)}, bf16[1408,512]{1,0:T(8,128)(2,1)}) custom-call(bf16[4096,512]{1,0:T(8,128)(2,1)} %get-tuple-element.34.h, bf16[4096,512]{1,0:T(8,128)(2,1)} %bitcast.40, bf16[4096,1408]{1,0:T(8,128)(2,1)} %get-tuple-element.35.act0, ...), custom_call_target="tpu_custom_call" | custom-call | tf_op jit(solution)/shard_map/both1/pallas_call | solution.py:402
  155.5 56.4 %backward0.1 = (bf16[512,1408]{1,0:T(8,128)(2,1)}, bf16[512,1408]{1,0:T(8,128)(2,1)}, bf16[32,1408]{1,0:T(8,128)(2,1)}, bf16[32,1408]{1,0:T(8,128)(2,1)}, bf16[8...) custom-call(bf16[4096,512]{1,0:T(8,128)(2,1)} %bitcast.33, bf16[4096,512]{1,0:T(8,128)(2,1)} %get-tuple-element.39.dh, ...), custom_call_target="tpu_custom_call" | custom-call | tf_op jit(solution)/shard_map/backward0/pallas_call | solution.py:414
  211.9 0.0 copy-start.1
  212.0 0.0 copy-start.6
  212.0 0.0 copy-start.7
  212.0 0.0 copy-start.8
  212.0 34.0 %scatter0.1 = (bf16[32,1408]{1,0:T(8,128)(2,1)}, bf16[32,1408]{1,0:T(8,128)(2,1)}, f32[8,128]{1,0:T(8,128)}) custom-call(bf16[8,2,32,1408]{3,2,1,0:T(8,128)(2,1)} %bitcast.41, bf16[8,2,32,1408]{3,2,1,0:T(8,128)(2,1)} %bitcast.42, bf16[32,1408]{1,0:T(8,128)(2,1)} %get-tuple-element.46.g0, bf16[32,1408]{1,0:T(8,128)(2,1)} %get-tuple-element.47.g1, ...), custom_call_target="tpu_custom_call" | custom-call | tf_op jit(solution)/shard_map/scatter0/pallas_call | solution.py:425
  246.0 0.0 copy-start
  246.0 0.0 copy-start.4
  246.0 0.0 copy-start.5
  246.0 0.0 copy-start.9
  246.0 0.0 copy-start.10
  246.1 1.4 reduce_sum.9
  248.1 0.0 copy-done.1
  248.1 0.0 copy-done.6
  248.1 0.0 copy-done.7
  248.2 0.0 copy-done.8
  248.2 1.9 fusion.2
  250.1 0.0 copy-start.2
  250.1 0.0 copy-start.3
  250.1 0.0 copy-start.11
  250.1 0.0 copy-start.12
  250.1 0.0 copy-start.13
  250.1 0.0 copy-done
  250.1 0.0 copy-done.4
  250.1 0.0 copy-done.5
  250.1 0.0 copy-done.9
  250.1 0.0 copy-done.10
  250.1 1.0 fusion.8
  251.2 0.0 copy-done.2
  251.2 0.0 copy-done.3
  251.2 0.2 copy-done.11
  251.3 0.3 copy-done.12
  251.6 0.0 copy-done.13
  251.6 1.0 fusion.5
Async XLA Ops:
  211.9 36.2 %copy-start.1 = (bf16[2,32,1408]{2,1,0:T(8,128)(2,1)S(1)}, bf16[2,32,1408]{2,1,0:T(8,128)(2,1)}, u32[]{:S(2)}) copy-start(bf16[2,32,1408]{2,1,0:T(8,128)(2,1)} %param.13) | copy-start | bytes 540676
  212.0 36.2 %copy-start.6 = (bf16[32,1408]{1,0:T(8,128)(2,1)S(1)}, bf16[32,1408]{1,0:T(8,128)(2,1)}, u32[]{:S(2)}) copy-start(bf16[32,1408]{1,0:T(8,128)(2,1)} %get-tuple-element.46.g0) | copy-start | bytes 270340
  212.0 36.2 %copy-start.7 = (f32[2,32,1408]{2,1,0:T(8,128)S(1)}, f32[2,32,1408]{2,1,0:T(8,128)}, u32[]{:S(2)}) copy-start(f32[2,32,1408]{2,1,0:T(8,128)} %param.19) | copy-start | bytes 1081348
  212.0 36.2 %copy-start.8 = (f32[2,32,1408]{2,1,0:T(8,128)S(1)}, f32[2,32,1408]{2,1,0:T(8,128)}, u32[]{:S(2)}) copy-start(f32[2,32,1408]{2,1,0:T(8,128)} %param.16) | copy-start | bytes 1081348
  246.0 4.1 %copy-start = (bf16[2,88,512]{2,1,0:T(8,128)(2,1)S(1)}, bf16[2,88,512]{2,1,0:T(8,128)(2,1)}, u32[]{:S(2)}) copy-start(bf16[2,88,512]{2,1,0:T(8,128)(2,1)} %param.15) | copy-start | bytes 540676
  246.0 4.1 %copy-start.4 = (bf16[88,512]{1,0:T(8,128)(2,1)S(1)}, bf16[88,512]{1,0:T(8,128)(2,1)}, u32[]{:S(2)}) copy-start(bf16[88,512]{1,0:T(8,128)(2,1)} %get-tuple-element.48.g2) | copy-start | bytes 270340
  246.0 4.1 %copy-start.5 = (bf16[88,512]{1,0:T(8,128)(2,1)S(1)}, bf16[88,512]{1,0:T(8,128)(2,1)}, u32[]{:S(2)}) copy-start(bf16[88,512]{1,0:T(8,128)(2,1)} %get-tuple-element.49.g3) | copy-start | bytes 270340
  246.0 4.1 %copy-start.9 = (f32[2,88,512]{2,1,0:T(8,128)S(1)}, f32[2,88,512]{2,1,0:T(8,128)}, u32[]{:S(2)}) copy-start(f32[2,88,512]{2,1,0:T(8,128)} %param.21) | copy-start | bytes 1081348
  246.0 4.1 %copy-start.10 = (f32[2,88,512]{2,1,0:T(8,128)S(1)}, f32[2,88,512]{2,1,0:T(8,128)}, u32[]{:S(2)}) copy-start(f32[2,88,512]{2,1,0:T(8,128)} %param.18) | copy-start | bytes 1081348
  250.1 1.1 copy-start.2
  250.1 1.1 copy-start.3
  250.1 1.3 copy-start.11
  250.1 1.6 copy-start.12
  250.1 1.6 copy-start.13

commit v2 on v1

v2 whole, which is shorter than its diff:
```python
import functools
import math

import jax
import jax.numpy as jnp
from jax import lax
from jax.experimental import pallas as pl
from jax.experimental.pallas import tpu as pltpu
from jax.sharding import PartitionSpec as P

F32, BF16 = jnp.float32, jnp.bfloat16
TILE = 512
VMEM_LIMIT = 60 << 20
MESH = pl.DeviceIdType.MESH


def dot(a, b):
    return jnp.dot(a, b, preferred_element_type=F32)


def norm_parts(h):
    wide = h.astype(F32)
    scale = lax.rsqrt(jnp.mean(wide * wide, -1, keepdims=True) + 1e-6)
    return wide, scale, (wide * scale).astype(BF16)


def sigmoid(x):
    return 0.5 * jnp.tanh(0.5 * x) + 0.5


class Place:
    def __init__(self, chips, groups=None):
        self.dp = me = lax.axis_index("dp")
        if groups is not None:
            rep, length = lax.axis_index("rep"), math.isqrt(groups)
            x, y = rep // length, rep % length
            self.parity = (x + y) % 2
            self.across = ((x + 1 - 2 * (x % 2)) * length + y, x * length + y + 1 - 2 * (y % 2))
        self.chips, self.half = chips, chips // 2
        self.z, self.c = me // 2, me % 2
        self.sibling = self.z * 2 + 1 - self.c

    def chip(self, offset):
        return lax.rem(self.z + offset + 2 * self.chips, self.chips)

    def beside(self, direction):
        return self.chip(direction) * 2 + self.c


def ident(device, group=None):
    return {"dp": device} if group is None else {"rep": group, "dp": device}


def meet(devices):
    barrier = pltpu.get_barrier_semaphore()
    for device in devices:
        pl.semaphore_signal(barrier, inc=1, device_id=ident(*device), device_id_type=MESH)
    pl.semaphore_wait(barrier, len(devices))


def remote(src, dst, send, recv, device, group=None):
    return pltpu.make_async_remote_copy(src_ref=src, dst_ref=dst, send_sem=send, recv_sem=recv, device_id=ident(device, group), device_id_type=MESH)


DIRECTIONS = (1, -1)


class Gather:
    PIECES = 4
    SIGNS = (1, -1, 1, -1)

    def __init__(self, place, layer, shards, gu, down, sems):
        self.p, self.shards, self.gu, self.down = place, [s.at[layer] for s in shards], gu, down
        self.ring_send, self.ring_recv, self.cross_send, self.cross_recv, self.side_send, self.side_recv, self.own_sem = sems
        self.rows, self.ff = self.shards[0].shape
        self.d = self.shards[2].shape[1]

    @staticmethod
    def scratch(chips):
        ring, dma = 2 * (chips // 2) * Gather.PIECES, pltpu.SemaphoreType.DMA
        return [dma((ring,)), dma((ring,)), dma((Gather.PIECES,)), dma((ring,)), dma((2,)), dma((2,)), dma((3,))]

    def goes(self, direction, step, m):
        return step < self.p.half - 1 or self.SIGNS[m] == direction

    def part(self, m, parity):
        if m < 2:
            half = self.rows // 2
            return pl.ds(pl.multiple_of(parity * half, half), half), slice(None)
        quarter = self.d // 4
        return slice(None), pl.ds(pl.multiple_of((2 * parity + m - 2) * quarter, quarter), quarter)

    def block(self, m, chip, core):
        return self.down.at[chip, core] if m >= 2 else self.gu.at[chip, core, :, m * self.ff : (m + 1) * self.ff]

    def piece(self, m, chip, parity):
        return self.block(m, chip, self.p.c).at[self.part(m, parity)]

    def source(self, direction, step, m, parity):
        if step == 0:
            return self.shards[min(m, 2)].at[self.part(m, parity)]
        return self.piece(m, self.p.chip(-direction * step), parity)

    def index(self, direction, step, m):
        return ((direction < 0) * self.p.half + step) * self.PIECES + m

    def ring(self, direction, step, m):
        p, k = self.p, self.index(direction, step, m)
        place = self.piece(m, p.chip(-direction * step), p.parity)
        return remote(self.source(direction, step, m, p.parity), place, self.ring_send.at[k], self.ring_recv.at[k], p.beside(direction))

    def cross(self, direction, step, m):
        p, k = self.p, self.index(direction, step, m)
        place = self.piece(m, p.chip(-direction * (step + 1)), p.parity)
        return remote(place, place, self.cross_send.at[m], self.cross_recv.at[k], p.dp, p.across[m % 2])

    def side(self, ref, m):
        return remote(ref, ref, self.side_send.at[m // 2], self.side_recv.at[m // 2], self.p.sibling)

    def own(self, m):
        return pltpu.make_async_copy(self.shards[m], self.block(m, self.p.z, self.p.c), self.own_sem.at[m])

    def start(self):
        p = self.p
        for m in range(self.PIECES):
            for direction in DIRECTIONS:
                if self.goes(direction, 0, m):
                    self.ring(direction, 0, m).start()
        for m in range(3):
            self.own(m).start()
            place = self.block(m, p.z, p.c)
            remote(self.shards[m], place, self.side_send.at[m // 2], self.side_recv.at[m // 2], p.sibling).start()

    def step(self, step, m):
        p = self.p
        for direction in DIRECTIONS:
            if self.goes(direction, step - 1, m):
                self.ring(direction, step - 1, m).wait_recv()
                if step < p.half and self.goes(direction, step, m):
                    self.ring(direction, step, m).start()
                self.cross(direction, step - 1, m).start()
                self.side(self.piece(m, p.chip(-direction * step), p.parity), m).start()

    def crossed(self, step, m):
        p = self.p
        for direction in DIRECTIONS:
            if self.goes(direction, step - 1, m):
                chip = p.chip(-direction * step)
                k = self.index(direction, step - 1, m)
                place = self.piece(m, chip, 1 - p.parity)
                remote(place, place, self.cross_send.at[m], self.cross_recv.at[k], p.dp, p.across[m % 2]).wait_recv()
                self.side(place, m).start()

    def finish(self):
        p = self.p
        for m in range(3):
            self.own(m).wait()
        for m, ref in ((0, self.gu), (2, self.down)):
            self.side(ref.at[:, 0], m).wait()
        for m in range(self.PIECES):
            sent = self.block(m, slice(0, p.chips - 1), 0).at[(slice(None), *self.first(m))]
            remote(sent, sent, self.cross_send.at[m], self.cross_recv.at[0], p.dp, p.across[m % 2]).wait_send()
            for direction in DIRECTIONS:
                for step in range(p.half):
                    if self.goes(direction, step, m):
                        self.ring(direction, step, m).wait_send()

    def first(self, m):
        return (slice(0, self.rows // 2), slice(None)) if m < 2 else (slice(None), slice(0, self.d // 4))


class Scatter:
    def __init__(self, place, terms, signs, scratch, in_hbm):
        self.p, self.terms, self.signs, self.in_hbm, n = place, terms, signs, in_hbm, len(terms)
        scratch = list(scratch)
        take = lambda k: [scratch.pop(0) for _ in range(k)]
        self.other, self.sent, self.came = take(n), take(n), take(n)
        self.own = take(n) if in_hbm else None
        self.pair_send, self.pair_recv, self.ring_send, self.ring_recv, self.own_sem = scratch

    @staticmethod
    def scratch(chips, shapes, in_hbm):
        steps, n, dma = chips // 2, len(shapes), pltpu.SemaphoreType.DMA
        blocks = [pltpu.VMEM((chips, *shape), BF16) for shape in shapes]
        slots = [pltpu.VMEM((2 * steps, *shape), BF16) for shape in shapes]
        return blocks + slots * 2 + blocks * in_hbm + [dma((n,)), dma((n,)), dma((2 * steps * n,)), dma((2 * steps * n,)), dma((n,))]

    def local(self, m):
        return pltpu.make_async_copy(self.terms[m].at[:, self.p.c], self.own[m], self.own_sem.at[m])

    def pair(self, m):
        return remote(self.terms[m].at[:, 1 - self.p.c], self.other[m], self.pair_send.at[m], self.pair_recv.at[m], self.p.sibling)

    def goes(self, direction, step, m):
        return step > 0 or self.signs[m] == direction

    def slot(self, direction, step):
        return (direction < 0) * self.p.half + step

    def ring(self, direction, step, m):
        slot = self.slot(direction, step)
        k = slot * len(self.terms) + m
        return remote(self.sent[m].at[slot], self.came[m].at[slot], self.ring_send.at[k], self.ring_recv.at[k], self.p.beside(direction))

    def exchange(self):
        for m in range(len(self.terms)):
            self.pair(m).start()
            if self.in_hbm:
                self.local(m).start()

    def mine(self, m, t):
        own = self.own[m][t] if self.in_hbm else self.terms[m][t, self.p.c]
        return own.astype(F32) + self.other[m][t].astype(F32)

    def step(self, step):
        for m in range(len(self.terms)):
            if step == 0:
                if self.in_hbm:
                    self.local(m).wait()
                self.pair(m).wait_recv()
            for direction in DIRECTIONS:
                if not self.goes(direction, step, m):
                    continue
                value = self.mine(m, self.p.chip(direction * (self.p.half - step)))
                if step > 0 and self.goes(direction, step - 1, m):
                    self.ring(direction, step - 1, m).wait_recv()
                    value = value + self.came[m][self.slot(direction, step - 1)].astype(F32)
                self.sent[m][self.slot(direction, step)] = value.astype(BF16)
                self.ring(direction, step, m).start()

    def result(self, m):
        last = self.p.half - 1
        value = self.mine(m, self.p.z)
        for direction in DIRECTIONS:
            self.ring(direction, last, m).wait_recv()
            value = value + self.came[m][self.slot(direction, last)].astype(F32)
        return value.astype(BF16)

    def finish(self):
        for m in range(len(self.terms)):
            self.pair(m).wait_send()
            for direction in DIRECTIONS:
                for step in range(self.p.half):
                    if self.goes(direction, step, m):
                        self.ring(direction, step, m).wait_send()


CHUNKS = (512, 512, 384)
SCHEDULE = {
    "first": (2, 3, 5, 7, 10),
    "second": (2, 4, 6, 8, 11),
    "chunk0": (4, 5, 6, 8, 10),
    "chunk1": (8, 9, 11),
}


def forward_kernel(chips, groups, x, s0, s1, s2, h_out, act_out, a_out, at_out, w0gu, w0d, w1gu, w1d, gu, down, keep_sem, *sems):
    i, n = pl.program_id(0), pl.num_programs(0)
    place = Place(chips, groups)
    ff = s0.shape[2]
    d = x.shape[1]
    half = len(sems) // 2
    one = Gather(place, 0, (s0, s1, s2), gu, down, sems[:half])
    two = Gather(place, 1, (s0, s1, s2), w1gu, w1d, sems[half:])
    keep = [pltpu.make_async_copy(src, dst, keep_sem.at[k]) for k, (src, dst) in enumerate(((gu, w0gu), (down, w0d)))]
    last = place.half
    pieces = range(Gather.PIECES)

    @pl.when(i == 0)
    def _():
        meet([(place.sibling,), (place.beside(1),), (place.beside(-1),), *[(place.dp, group) for group in place.across]])
        one.start()
        for step in range(1, last + 1):
            for m in pieces:
                one.step(step, m)
                if step > 1:
                    one.crossed(step - 1, m)
        two.start()
        for m in pieces:
            one.crossed(last, m)
        one.finish()
        for copy in keep:
            copy.start()

    for step in range(1, last + 1):

        @pl.when(i == step)
        def _(step=step):
            for m in pieces:
                two.step(step, m)
                if step > 1:
                    two.crossed(step - 1, m)

    @pl.when(i == last + 1)
    def _():
        for m in pieces:
            two.crossed(last, m)

    h = x[...]
    _, _, a = norm_parts(h)
    a_out[...] = a
    at_out[...] = a.T
    both = dot(a, gu[...].reshape(d, 2 * ff))
    gate, up = both[:, :ff], both[:, ff:]
    act = (gate * sigmoid(gate) * up).astype(BF16)
    act_out[...] = act
    out = dot(act, down[...].reshape(ff, d)).astype(BF16)
    h_out[...] = (h.astype(F32) + out.astype(F32)).astype(BF16)

    @pl.when(i == n - 1)
    def _():
        two.finish()
        for copy in keep:
            copy.wait()


def act_backward(gate, up, by_act):
    by_act = by_act.astype(BF16).astype(F32)
    sig = sigmoid(gate)
    silu = gate * sig
    act = (silu * up).astype(BF16)
    by_up = (by_act * silu).astype(BF16)
    by_gate = (by_act * up * (sig + silu * (1.0 - sig))).astype(BF16)
    return act, by_gate, by_up


def both_kernel(h, dy, act0, wgu, wd, dh_out, gg, gu, gd, gd0, wgut, wdt, by_gu, agu, ad, ad0):
    i, n = pl.program_id(0), pl.num_programs(0)
    ff = wd.shape[0]

    @pl.when(i == 0)
    def _():
        wgut[...] = wgu[...].T
        wdt[...] = wd[...].T
        for acc in (agu, ad, ad0):
            acc[...] = jnp.zeros_like(acc)

    by_out = dy[...]
    wide, scale, a = norm_parts(h[...])
    both = dot(a, wgu[...])
    act, by_gate, by_up = act_backward(both[:, :ff], both[:, ff:], dot(by_out, wdt[...]))
    by_gu[:, :ff] = by_gate
    by_gu[:, ff:] = by_up
    by_a = dot(by_gu[...], wgut[...]).astype(BF16).astype(F32)
    agu[...] += dot(a.T, by_gu[...])
    ad[...] += dot(by_out.T, act)
    by_wide = by_a * scale - wide * (scale * scale * scale * jnp.mean(by_a * wide, -1, keepdims=True))
    by_h = (by_out.astype(F32) + by_wide.astype(BF16).astype(F32)).astype(BF16)
    dh_out[...] = by_h
    ad0[...] += dot(by_h.T, act0[...])

    @pl.when(i == n - 1)
    def _():
        gg[...] = agu[:, :ff].astype(BF16)
        gu[...] = agu[:, ff:].astype(BF16)
        gd[...] = ad[...].astype(BF16).T
        gd0[...] = ad0[...].astype(BF16).T


def add_up(squares, g):
    g = g.astype(F32)
    g = (g * g).reshape(g.shape[0] // 8, 8, g.shape[1]).sum(0)
    return squares + sum(g[:, k : k + 128] for k in range(0, g.shape[1], 128))


def backward_kernel(chips, tiles, sizes, a, at, dh, wgu, wd, t0, t1, t2, t3, rg, ru, rg1, ru1, rd1, rd0, total, wdt, ag, au, squares, part, parts, part_send, part_recv, *scratch):
    i = pl.program_id(0)
    place = Place(chips)
    group = 2 * chips
    me = lax.axis_index("dp")
    ff = wd.shape[0]
    scratch = list(scratch)
    take = lambda k: [scratch.pop(0) for _ in range(k)]
    hbm_count, chunk_count = 4 * 2 + 5, 3 * 2 + 5
    first = Scatter(place, (t0, t1), (1, -1), take(hbm_count), True)
    second = Scatter(place, (t2, t3), (1, -1), take(hbm_count), True)
    chunks = []
    for _ in sizes:
        terms = take(2)
        chunks.append(Scatter(place, terms, (1, -1), take(chunk_count), False))
    steps = place.half
    starts = [sum(sizes[:k]) for k in range(len(sizes))]

    def settle(scatter, outs):
        sums = squares[...]
        for m, out in enumerate(outs):
            value = scatter.result(m)
            out[...] = value
            sums = add_up(sums, value)
        squares[...] = sums
        scatter.finish()

    def chunk_outs(k):
        return [r.at[:, starts[k] : starts[k] + sizes[k]] for r in (rg, ru)]

    events = []
    for name, scatter, outs in (("first", first, (rg1, ru1)), ("second", second, (rd1, rd0))):
        times = SCHEDULE[name]
        events += [(times[s], functools.partial(scatter.step, s)) for s in range(steps)]
        events.append((times[steps], functools.partial(settle, scatter, outs)))
    for k in range(len(sizes) - 1):
        times = SCHEDULE[f"chunk{k}"]
        for s in range(len(times) - 1):
            events.append((times[s + 1], functools.partial(chunks[k].step, s) if s < steps else functools.partial(settle, chunks[k], chunk_outs(k))))

    def clear():
        ag[...] = jnp.zeros_like(ag)
        au[...] = jnp.zeros_like(au)

    @pl.when(i == 0)
    def _():
        others = [lax.rem(me + k, group) for k in range(1, group)]
        meet([(other,) for other in others])
        first.exchange()
        second.exchange()
        squares[...] = jnp.zeros_like(squares)
        wdt[...] = wd[...].T
        clear()

    for when in sorted({when for when, _ in events}):

        @pl.when(i == when)
        def _(now=when):
            for when, act in events:
                if when == now:
                    act()

    for k, size in enumerate(sizes):

        @pl.when(i // tiles == k)
        def _(k=k, size=size):
            cols = slice(starts[k], starts[k] + size)
            by_out = dh[...]
            gate, up = dot(a[...], wgu[:, cols]), dot(a[...], wgu[:, ff + cols.start : ff + cols.stop])
            _, by_gate, by_up = act_backward(gate, up, dot(by_out, wdt[:, cols]))
            ag[:, :size] += dot(at[...], by_gate)
            au[:, :size] += dot(at[...], by_up)

        @pl.when(i == (k + 1) * tiles - 1)
        def _(k=k, size=size):
            for term, acc in zip(chunks[k].terms, (ag, au)):
                term[...] = acc[:, :size].astype(BF16).reshape(term.shape)
            chunks[k].exchange()
            clear()

    @pl.when(i == len(sizes) * tiles - 1)
    def _():
        done = [len(SCHEDULE[f"chunk{k}"]) - 1 for k in range(len(sizes) - 1)] + [0]
        for s in range(steps):
            for k, chunk in enumerate(chunks):
                if done[k] <= steps and done[k] + s < steps:
                    chunk.step(done[k] + s)
                elif done[k] <= steps and done[k] + s == steps:
                    settle(chunk, chunk_outs(k))
        settle(chunks[-1], chunk_outs(len(sizes) - 1))
        part[...] = squares[...]
        copies = [remote(part, parts.at[group - k - 1], part_send.at[k - 1], part_recv.at[group - k - 1], lax.rem(me + k, group)) for k in range(1, group)]
        for copy in copies:
            copy.start()
        sums = squares[...]
        for k in range(1, group):
            remote(part, parts.at[k - 1], part_send.at[k - 1], part_recv.at[k - 1], lax.rem(me + k, group)).wait_recv()
            sums = sums + parts[k - 1]
        for copy in copies:
            copy.wait_send()
        total[...] = sums


def step_kernel(count, total, *refs):
    ws, ms, vs, gs, outs = refs[:3], refs[3:6], refs[6:9], refs[9:15], refs[15:]
    squares = jnp.sum(jnp.sum(total[...], 0, keepdims=True), 1, keepdims=True)
    factor = jnp.minimum(1.0, 0.5 * lax.rsqrt(squares / count + 1e-30))
    for k in range(3):
        for layer in range(2):
            g = gs[2 * k + layer][...].astype(F32) * factor
            w, m, v = adamw(ws[k][layer].astype(F32), ms[k][layer], vs[k][layer], g)
            outs[k][layer], outs[3 + k][layer], outs[6 + k][layer] = w, m, v


def whole(shape=None):
    return pl.BlockSpec(memory_space=pltpu.VMEM) if shape is None else pl.BlockSpec(shape, lambda i: (0,) * len(shape), pipeline_mode=pl.Buffered(1))


def params(collective=None, **more):
    if collective is not None:
        more.update(collective_id=collective, has_side_effects=True)
    return pltpu.CompilerParams(vmem_limit_bytes=VMEM_LIMIT, **more)


def adamw(w, m, v, g):
    m = 0.9 * m + 0.1 * g
    v = 0.95 * v + 0.05 * g * g
    step = m * lax.rsqrt(v + 1e-8) + 0.1 * w
    return (w - 0.02 * step).astype(BF16), m, v


def solution(mesh):
    group, groups = mesh.shape["dp"], mesh.shape["rep"]
    chips = group // 2
    any_space = pl.BlockSpec(memory_space=pl.ANY)

    def step(x, dy, *arrays):
        weights, ms, vs = (arrays[i : i + 3] for i in (0, 3, 6))
        x, dy = x[0], dy[0]
        tokens, d = x.shape
        tiles = tokens // TILE
        rows = [(w.shape[1], w.shape[2]) for w in weights]
        ff = rows[0][1]
        d_ff = (d, ff)
        gu_blocks = jax.ShapeDtypeStruct((chips, 2, rows[0][0], 2 * ff), BF16)
        down_blocks = jax.ShapeDtypeStruct((chips, 2, *rows[2]), BF16)

        def split(g, m):
            return g.reshape(chips, 2, *rows[m])

        narrow = pl.BlockSpec((TILE, d), lambda i: (i, 0))
        broad = pl.BlockSpec((TILE, ff), lambda i: (i, 0))
        weight_specs = [whole((d, 2 * ff)), whole((ff, d))]
        tokens_d = jax.ShapeDtypeStruct((tokens, d), BF16)
        tokens_ff = jax.ShapeDtypeStruct((tokens, ff), BF16)
        dma = pltpu.SemaphoreType.DMA
        h1, act0, a0, a0t, *full = pl.pallas_call(
            functools.partial(forward_kernel, chips, groups),
            grid=(tiles,),
            out_shape=[tokens_d, tokens_ff, tokens_d, jax.ShapeDtypeStruct((d, tokens), BF16), *[gu_blocks, down_blocks] * 2],
            in_specs=[narrow, *[whole(w.shape) for w in weights]],
            out_specs=[narrow, broad, narrow, pl.BlockSpec((d, TILE), lambda i: (0, i)), *[any_space] * 4],
            scratch_shapes=[pltpu.VMEM(gu_blocks.shape, BF16), pltpu.VMEM(down_blocks.shape, BF16), dma((2,))] + Gather.scratch(chips) * 2,
            compiler_params=params(1, dimension_semantics=("arbitrary",)),
            name="forward0",
        )(x, *weights)
        w0, w1 = ([full[k].reshape(d, 2 * ff), full[k + 1].reshape(ff, d)] for k in (0, 2))

        wide = jax.ShapeDtypeStruct(d_ff, BF16)
        tall = jax.ShapeDtypeStruct((ff, d), BF16)
        dh, gg1, gu1, gd1, gd0 = pl.pallas_call(
            both_kernel,
            grid=(tiles,),
            out_shape=[tokens_d, wide, wide, tall, tall],
            in_specs=[narrow, narrow, broad, *weight_specs],
            out_specs=[narrow, whole(d_ff), whole(d_ff), whole((ff, d)), whole((ff, d))],
            scratch_shapes=[pltpu.VMEM((2 * ff, d), BF16), pltpu.VMEM(d_ff, BF16), pltpu.VMEM((TILE, 2 * ff), BF16)]
            + [pltpu.VMEM((d, 2 * ff), F32)]
            + [pltpu.VMEM(d_ff, F32)] * 2,
            compiler_params=params(dimension_semantics=("arbitrary",)),
            name="both1",
        )(h1, dy, act0, *w1)

        blocks = [jax.ShapeDtypeStruct(r, BF16) for r in rows]
        sizes = CHUNKS
        scratch = [pltpu.VMEM(d_ff, BF16)] + [pltpu.VMEM((d, max(sizes)), F32)] * 2
        scratch += [pltpu.VMEM((8, 128), F32)] * 2 + [pltpu.VMEM((group - 1, 8, 128), F32)] + [dma((group - 1,))] * 2
        scratch += Scatter.scratch(chips, rows[:2], True) + Scatter.scratch(chips, [rows[2]] * 2, True)
        for size in sizes:
            block = (rows[0][0], size)
            scratch += [pltpu.VMEM((chips, 2, *block), BF16)] * 2 + Scatter.scratch(chips, [block] * 2, False)
        tiles = tokens // (2 * TILE)
        again = pl.BlockSpec((2 * TILE, d), lambda i: (lax.rem(i, tiles), 0))
        across = pl.BlockSpec((d, 2 * TILE), lambda i: (0, lax.rem(i, tiles)))
        rg0, ru0, rg1, ru1, rd1, rd0, total = pl.pallas_call(
            functools.partial(backward_kernel, chips, tiles, sizes),
            grid=(len(sizes) * tiles,),
            out_shape=[blocks[0], blocks[1], *blocks, blocks[2], jax.ShapeDtypeStruct((8, 128), F32)],
            in_specs=[again, across, again, *weight_specs, *[any_space] * 4],
            out_specs=[whole(r) for r in (rows[0], rows[1], *rows, rows[2], (8, 128))],
            scratch_shapes=scratch,
            compiler_params=params(2, dimension_semantics=("arbitrary",)),
            name="backward0",
        )(a0, a0t, dh, *w0, split(gg1, 0), split(gu1, 1), split(gd1, 2), split(gd0, 2))

        count = group * sum(w.size for w in weights)
        new = [jax.ShapeDtypeStruct(w.shape, t) for t in (BF16, F32, F32) for w in weights]
        return tuple(
            pl.pallas_call(
                functools.partial(step_kernel, count),
                out_shape=new,
                in_specs=[whole()] * 16,
                out_specs=[whole()] * 9,
                compiler_params=params(),
                name="adamw",
            )(total, *weights, *ms, *vs, rg0, rg1, ru0, ru1, rd0, rd1)
        )

    states, cut = P(("rep", "dp"), None, None), P(None, "dp", None)
    return jax.shard_map(
        step,
        mesh=mesh,
        in_specs=(states, states) + (cut,) * 9,
        out_specs=(P("rep", "dp", None),) * 9,
        check_vma=False,
    )
```

time: 253 us -> 214 us (0.85)
  Pallas kernels: 242 us -> 214 us
  other arithmetic: 5.3 us -> 0 us
  local copies, waits for them, and re-layouts: 3.9 us -> 0 us
    pallas_call x4 -> x3, Pallas kernels: 164 us -> 142 us  [the longest x1 78.6 us: step(): pl.pallas_call(functools.partial(backward_kernel, chips, tiles, sizes), g...]
    pallas_call x1, Pallas kernels: 77.4 us -> 71.1 us  [step(): pl.pallas_call(both_kernel, grid=(tiles,), out_shape=[tokens_d, wide, wid...]
    convert_element_type x3 -> x0, other arithmetic: 3.92 us -> none  [adamw(): return ((w - 0.02 * step).astype(BF16), m, v)]
    squeeze x2 -> x0, local copies, waits for them, and re-layouts: 3.37 us -> none  [step(): shards = [[w[layer] for w in weights] for layer in range(2)]]
where the time goes in v2:
time: 214 us
  Pallas kernels  214 us (100%)
    pallas_call x1, Pallas kernels, step(): pl.pallas_call(functools.partial(backward_kernel, chips, tiles, sizes), g...  78.6 us
    pallas_call x1, Pallas kernels, step(): pl.pallas_call(both_kernel, grid=(tiles,), out_shape=[tokens_d, wide, wid...  71.1 us
    pallas_call x1, Pallas kernels, step(): pl.pallas_call(functools.partial(forward_kernel, chips, groups), grid=(ti...  60 us

profile of v2, /device:TPU:21, one launch (start us, length us, event | category | flops | bytes accessed | tf_op | source)
XLA Modules:
  0.0 214.3 jit_solution(9729348840772865372)
XLA Ops:
  0.6 60.0 %forward0.1 = (bf16[4096,512]{1,0:T(8,128)(2,1)}, bf16[4096,1408]{1,0:T(8,128)(2,1)}, bf16[4096,512]{1,0:T(8,128)(2,1)}, bf16[512,4096]{1,0:T(8,128)(2,1)}, bf16...) custom-call(bf16[4096,512]{1,0:T(8,128)(2,1)} %bitcast.10, ...), custom_call_target="tpu_custom_call" | custom-call | tf_op jit(solution)/shard_map/forward0/pallas_call | solution.py:522
  60.6 71.1 %both1.1 = (bf16[4096,512]{1,0:T(8,128)(2,1)}, bf16[512,1408]{1,0:T(8,128)(2,1)}, bf16[512,1408]{1,0:T(8,128)(2,1)}, bf16[1408,512]{1,0:T(8,128)(2,1)}, bf16[1408,512]{1,0:T(8,128)(2,1)}) custom-call(bf16[4096,512]{1,0:T(8,128)(2,1)} %get-tuple-element.31.h, bf16[4096,512]{1,0:T(8,128)(2,1)} %bitcast.11, bf16[4096,1408]{1,0:T(8,128)(2,1)} %get-tuple-element.32.act0, ...), custom_call_target="tpu_custom_call" | custom-call | tf_op jit(solution)/shard_map/both1/pallas_call | solution.py:536
  131.7 78.6 %backward0.1 = (bf16[32,1408]{1,0:T(8,128)(2,1)}, bf16[32,1408]{1,0:T(8,128)(2,1)}, bf16[32,1408]{1,0:T(8,128)(2,1)}, bf16[32,1408]{1,0:T(8,128)(2,1)}, bf16[88,...) custom-call(bf16[4096,512]{1,0:T(8,128)(2,1)} %get-tuple-element.29.a, ...), custom_call_target="tpu_custom_call" | custom-call | tf_op jit(solution)/shard_map/backward0/pallas_call | solution.py:560
  210.3 3.8 %adamw.1 = (bf16[2,32,1408]{2,1,0:T(8,128)(2,1)}, bf16[2,32,1408]{2,1,0:T(8,128)(2,1)}, bf16[2,88,512]{2,1,0:T(8,128)(2,1)}, f32[2,32,1408]{2,1,0:T(8,128)}, f32...) custom-call(f32[8,128]{1,0:T(8,128)} %get-tuple-element.42.total, ...), custom_call_target="tpu_custom_call" | custom-call | tf_op jit(solution)/shard_map/adamw/pallas_call | solution.py:574

commit v3 on v2

--- a/solution.py
+++ b/solution.py
@@ -247,10 +247,11 @@
 
 CHUNKS = (512, 512, 384)
 SCHEDULE = {
-    "first": (2, 3, 5, 7, 10),
-    "second": (2, 4, 6, 8, 11),
-    "chunk0": (4, 5, 6, 8, 10),
-    "chunk1": (8, 9, 11),
+    "first": (2, 4, 6, 8, 10),
+    "second": (3, 5, 7, 9, 11),
+    "third": (5, 6, 8, 9, 11),
+    "run0": (8, 10, 11, 12, 14),
+    "run1": (13, 14, 15),
 }
 
 
@@ -283,18 +284,14 @@
             copy.start()
 
     for step in range(1, last + 1):
-
-        @pl.when(i == step)
-        def _(step=step):
-            for m in pieces:
-                two.step(step, m)
-                if step > 1:
-                    two.crossed(step - 1, m)
-
-    @pl.when(i == last + 1)
-    def _():
-        for m in pieces:
-            two.crossed(last, m)
+        for late, some in enumerate(((0, 1), (2, 3))):
+
+            @pl.when(i == min(2 * step - 1 + late, 2 * last - 1))
+            def _(step=step, some=some):
+                for m in some:
+                    two.step(step, m)
+                    if step > 1:
+                        two.crossed(step - 1, m)
 
     h = x[...]
     _, _, a = norm_parts(h)
@@ -309,6 +306,8 @@
 
     @pl.when(i == n - 1)
     def _():
+        for m in pieces:
+            two.crossed(last, m)
         two.finish()
         for copy in keep:
             copy.wait()
@@ -324,7 +323,7 @@
     return act, by_gate, by_up
 
 
-def both_kernel(h, dy, act0, wgu, wd, dh_out, gg, gu, gd, gd0, wgut, wdt, by_gu, agu, ad, ad0):
+def both_kernel(h, dy, wgu, wd, dh_out, dht_out, gg, gu, gd, wgut, wdt, by_gu, agu, ad):
     i, n = pl.program_id(0), pl.num_programs(0)
     ff = wd.shape[0]
 
@@ -332,7 +331,7 @@
     def _():
         wgut[...] = wgu[...].T
         wdt[...] = wd[...].T
-        for acc in (agu, ad, ad0):
+        for acc in (agu, ad):
             acc[...] = jnp.zeros_like(acc)
 
     by_out = dy[...]
@@ -347,14 +346,13 @@
     by_wide = by_a * scale - wide * (scale * scale * scale * jnp.mean(by_a * wide, -1, keepdims=True))
     by_h = (by_out.astype(F32) + by_wide.astype(BF16).astype(F32)).astype(BF16)
     dh_out[...] = by_h
-    ad0[...] += dot(by_h.T, act0[...])
+    dht_out[...] = by_h.T
 
     @pl.when(i == n - 1)
     def _():
         gg[...] = agu[:, :ff].astype(BF16)
         gu[...] = agu[:, ff:].astype(BF16)
         gd[...] = ad[...].astype(BF16).T
-        gd0[...] = ad0[...].astype(BF16).T
 
 
 def add_up(squares, g):
@@ -363,7 +361,7 @@
     return squares + sum(g[:, k : k + 128] for k in range(0, g.shape[1], 128))
 
 
-def backward_kernel(chips, tiles, sizes, a, at, dh, wgu, wd, t0, t1, t2, t3, rg, ru, rg1, ru1, rd1, rd0, total, wdt, ag, au, squares, part, parts, part_send, part_recv, *scratch):
+def backward_kernel(chips, tiles, sizes, a, at, dh, dht, act0, wgu, wd, t0, t1, t2, rg, ru, rg1, ru1, rd1, rd0, total, wdt, ad, ag, au, squares, part, parts, part_send, part_recv, *scratch):
     i = pl.program_id(0)
     place = Place(chips)
     group = 2 * chips
@@ -371,13 +369,13 @@
     ff = wd.shape[0]
     scratch = list(scratch)
     take = lambda k: [scratch.pop(0) for _ in range(k)]
-    hbm_count, chunk_count = 4 * 2 + 5, 3 * 2 + 5
-    first = Scatter(place, (t0, t1), (1, -1), take(hbm_count), True)
-    second = Scatter(place, (t2, t3), (1, -1), take(hbm_count), True)
+    first = Scatter(place, (t0, t1), (1, -1), take(4 * 2 + 5), True)
+    second = Scatter(place, (t2,), (1,), take(4 + 5), True)
+    third = Scatter(place, take(1), (-1,), take(3 + 5), False)
     chunks = []
     for _ in sizes:
         terms = take(2)
-        chunks.append(Scatter(place, terms, (1, -1), take(chunk_count), False))
+        chunks.append(Scatter(place, terms, (1, -1), take(3 * 2 + 5), False))
     steps = place.half
     starts = [sum(sizes[:k]) for k in range(len(sizes))]
 
@@ -394,14 +392,13 @@
         return [r.at[:, starts[k] : starts[k] + sizes[k]] for r in (rg, ru)]
 
     events = []
-    for name, scatter, outs in (("first", first, (rg1, ru1)), ("second", second, (rd1, rd0))):
+    for name, scatter, outs in (("first", first, (rg1, ru1)), ("second", second, (rd1,)), ("third", third, (rd0,))):
         times = SCHEDULE[name]
         events += [(times[s], functools.partial(scatter.step, s)) for s in range(steps)]
         events.append((times[steps], functools.partial(settle, scatter, outs)))
     for k in range(len(sizes) - 1):
-        times = SCHEDULE[f"chunk{k}"]
-        for s in range(len(times) - 1):
-            events.append((times[s + 1], functools.partial(chunks[k].step, s) if s < steps else functools.partial(settle, chunks[k], chunk_outs(k))))
+        for s, when in enumerate(SCHEDULE[f"run{k}"]):
+            events.append((when, functools.partial(chunks[k].step, s) if s < steps else functools.partial(settle, chunks[k], chunk_outs(k))))
 
     def clear():
         ag[...] = jnp.zeros_like(ag)
@@ -416,6 +413,7 @@
         squares[...] = jnp.zeros_like(squares)
         wdt[...] = wd[...].T
         clear()
+        ad[...] = jnp.zeros_like(ad)
 
     for when in sorted({when for when, _ in events}):
 
@@ -425,9 +423,19 @@
                 if when == now:
                     act()
 
+    @pl.when(i < tiles)
+    def _():
+        ad[...] += dot(dht[...], act0[...])
+
+    @pl.when(i == tiles - 1)
+    def _():
+        term = third.terms[0]
+        term[...] = ad[...].T.reshape(term.shape).astype(BF16)
+        third.exchange()
+
     for k, size in enumerate(sizes):
 
-        @pl.when(i // tiles == k)
+        @pl.when(i // tiles == k + 1)
         def _(k=k, size=size):
             cols = slice(starts[k], starts[k] + size)
             by_out = dh[...]
@@ -436,16 +444,16 @@
             ag[:, :size] += dot(at[...], by_gate)
             au[:, :size] += dot(at[...], by_up)
 
-        @pl.when(i == (k + 1) * tiles - 1)
+        @pl.when(i == (k + 2) * tiles - 1)
         def _(k=k, size=size):
             for term, acc in zip(chunks[k].terms, (ag, au)):
                 term[...] = acc[:, :size].astype(BF16).reshape(term.shape)
             chunks[k].exchange()
             clear()
 
-    @pl.when(i == len(sizes) * tiles - 1)
-    def _():
-        done = [len(SCHEDULE[f"chunk{k}"]) - 1 for k in range(len(sizes) - 1)] + [0]
+    @pl.when(i == (len(sizes) + 1) * tiles - 1)
+    def _():
+        done = [len(SCHEDULE[f"run{k}"]) for k in range(len(sizes) - 1)] + [0]
         for s in range(steps):
             for k, chunk in enumerate(chunks):
                 if done[k] <= steps and done[k] + s < steps:
@@ -518,13 +526,15 @@
         weight_specs = [whole((d, 2 * ff)), whole((ff, d))]
         tokens_d = jax.ShapeDtypeStruct((tokens, d), BF16)
         tokens_ff = jax.ShapeDtypeStruct((tokens, ff), BF16)
+        tokens_t = jax.ShapeDtypeStruct((d, tokens), BF16)
+        narrow_t = pl.BlockSpec((d, TILE), lambda i: (0, i))
         dma = pltpu.SemaphoreType.DMA
         h1, act0, a0, a0t, *full = pl.pallas_call(
             functools.partial(forward_kernel, chips, groups),
             grid=(tiles,),
-            out_shape=[tokens_d, tokens_ff, tokens_d, jax.ShapeDtypeStruct((d, tokens), BF16), *[gu_blocks, down_blocks] * 2],
+            out_shape=[tokens_d, tokens_ff, tokens_d, tokens_t, *[gu_blocks, down_blocks] * 2],
             in_specs=[narrow, *[whole(w.shape) for w in weights]],
-            out_specs=[narrow, broad, narrow, pl.BlockSpec((d, TILE), lambda i: (0, i)), *[any_space] * 4],
+            out_specs=[narrow, broad, narrow, narrow_t, *[any_space] * 4],
             scratch_shapes=[pltpu.VMEM(gu_blocks.shape, BF16), pltpu.VMEM(down_blocks.shape, BF16), dma((2,))] + Gather.scratch(chips) * 2,
             compiler_params=params(1, dimension_semantics=("arbitrary",)),
             name="forward0",
@@ -533,40 +543,49 @@
 
         wide = jax.ShapeDtypeStruct(d_ff, BF16)
         tall = jax.ShapeDtypeStruct((ff, d), BF16)
-        dh, gg1, gu1, gd1, gd0 = pl.pallas_call(
+        dh, dht, gg1, gu1, gd1 = pl.pallas_call(
             both_kernel,
             grid=(tiles,),
-            out_shape=[tokens_d, wide, wide, tall, tall],
-            in_specs=[narrow, narrow, broad, *weight_specs],
-            out_specs=[narrow, whole(d_ff), whole(d_ff), whole((ff, d)), whole((ff, d))],
+            out_shape=[tokens_d, tokens_t, wide, wide, tall],
+            in_specs=[narrow, narrow, *weight_specs],
+            out_specs=[narrow, narrow_t, whole(d_ff), whole(d_ff), whole((ff, d))],
             scratch_shapes=[pltpu.VMEM((2 * ff, d), BF16), pltpu.VMEM(d_ff, BF16), pltpu.VMEM((TILE, 2 * ff), BF16)]
             + [pltpu.VMEM((d, 2 * ff), F32)]
-            + [pltpu.VMEM(d_ff, F32)] * 2,
+            + [pltpu.VMEM(d_ff, F32)],
             compiler_params=params(dimension_semantics=("arbitrary",)),
             name="both1",
-        )(h1, dy, act0, *w1)
+        )(h1, dy, *w1)
 
         blocks = [jax.ShapeDtypeStruct(r, BF16) for r in rows]
         sizes = CHUNKS
-        scratch = [pltpu.VMEM(d_ff, BF16)] + [pltpu.VMEM((d, max(sizes)), F32)] * 2
+        scratch = [pltpu.VMEM(d_ff, BF16), pltpu.VMEM(d_ff, F32)] + [pltpu.VMEM((d, max(sizes)), F32)] * 2
         scratch += [pltpu.VMEM((8, 128), F32)] * 2 + [pltpu.VMEM((group - 1, 8, 128), F32)] + [dma((group - 1,))] * 2
-        scratch += Scatter.scratch(chips, rows[:2], True) + Scatter.scratch(chips, [rows[2]] * 2, True)
+        scratch += Scatter.scratch(chips, rows[:2], True) + Scatter.scratch(chips, [rows[2]], True)
+        scratch += [pltpu.VMEM((chips, 2, *rows[2]), BF16)] + Scatter.scratch(chips, [rows[2]], False)
         for size in sizes:
             block = (rows[0][0], size)
             scratch += [pltpu.VMEM((chips, 2, *block), BF16)] * 2 + Scatter.scratch(chips, [block] * 2, False)
         tiles = tokens // (2 * TILE)
-        again = pl.BlockSpec((2 * TILE, d), lambda i: (lax.rem(i, tiles), 0))
-        across = pl.BlockSpec((d, 2 * TILE), lambda i: (0, lax.rem(i, tiles)))
+
+        def later(i):
+            return jnp.where(i < tiles, 0, lax.rem(i, tiles))
+
+        def early(i):
+            return jnp.minimum(i, tiles - 1)
+
+        again = pl.BlockSpec((2 * TILE, d), lambda i: (later(i), 0))
+        across = pl.BlockSpec((d, 2 * TILE), lambda i: (0, later(i)))
+        once = [pl.BlockSpec((d, 2 * TILE), lambda i: (0, early(i))), pl.BlockSpec((2 * TILE, ff), lambda i: (early(i), 0))]
         rg0, ru0, rg1, ru1, rd1, rd0, total = pl.pallas_call(
             functools.partial(backward_kernel, chips, tiles, sizes),
-            grid=(len(sizes) * tiles,),
+            grid=((len(sizes) + 1) * tiles,),
             out_shape=[blocks[0], blocks[1], *blocks, blocks[2], jax.ShapeDtypeStruct((8, 128), F32)],
-            in_specs=[again, across, again, *weight_specs, *[any_space] * 4],
+            in_specs=[again, across, again, *once, *weight_specs, *[any_space] * 3],
             out_specs=[whole(r) for r in (rows[0], rows[1], *rows, rows[2], (8, 128))],
             scratch_shapes=scratch,
             compiler_params=params(2, dimension_semantics=("arbitrary",)),
             name="backward0",
-        )(a0, a0t, dh, *w0, split(gg1, 0), split(gu1, 1), split(gd1, 2), split(gd0, 2))
+        )(a0, a0t, dh, dht, act0, *w0, split(gg1, 0), split(gu1, 1), split(gd1, 2))
 
         count = group * sum(w.size for w in weights)
         new = [jax.ShapeDtypeStruct(w.shape, t) for t in (BF16, F32, F32) for w in weights]

time: 214 us -> 220 us (1.028)
  Pallas kernels: 214 us -> 219 us
    pallas_call x1, Pallas kernels: 78.6 us -> 92 us  [step(): pl.pallas_call(functools.partial(backward_kernel, chips, tiles, sizes), g...]
    pallas_call x1, Pallas kernels: 71.1 us -> 63.7 us  [step(): pl.pallas_call(both_kernel, grid=(tiles,), out_shape=[tokens_d, tokens_t,...]
where the time goes in v3:
time: 220 us
  Pallas kernels  219 us (100%)
    pallas_call x1, Pallas kernels, step(): pl.pallas_call(functools.partial(backward_kernel, chips, tiles, sizes), g...  92 us
    pallas_call x1, Pallas kernels, step(): pl.pallas_call(both_kernel, grid=(tiles,), out_shape=[tokens_d, tokens_t,...  63.7 us
    pallas_call x1, Pallas kernels, step(): pl.pallas_call(functools.partial(forward_kernel, chips, groups), grid=(ti...  59.4 us

profile of v3, /device:TPU:21, one launch (start us, length us, event | category | flops | bytes accessed | tf_op | source)
XLA Modules:
  0.0 219.7 jit_solution(7753230112065610301)
XLA Ops:
  0.6 59.4 %forward0.1 = (bf16[4096,512]{1,0:T(8,128)(2,1)}, bf16[4096,1408]{1,0:T(8,128)(2,1)}, bf16[4096,512]{1,0:T(8,128)(2,1)}, bf16[512,4096]{1,0:T(8,128)(2,1)}, bf16...) custom-call(bf16[4096,512]{1,0:T(8,128)(2,1)} %bitcast.10, ...), custom_call_target="tpu_custom_call" | custom-call | tf_op jit(solution)/shard_map/forward0/pallas_call | solution.py:532
  60.1 63.7 %both1.1 = (bf16[4096,512]{1,0:T(8,128)(2,1)}, bf16[512,4096]{1,0:T(8,128)(2,1)}, bf16[512,1408]{1,0:T(8,128)(2,1)}, bf16[512,1408]{1,0:T(8,128)(2,1)}, bf16[1408,512]{1,0:T(8,128)(2,1)}) custom-call(bf16[4096,512]{1,0:T(8,128)(2,1)} %get-tuple-element.31.h, bf16[4096,512]{1,0:T(8,128)(2,1)} %bitcast.9, bf16[512,2816]{1,0:T(8,128)(2,1)} %bitcast.12, ...), custom_call_target="tpu_custom_call" | custom-call | tf_op jit(solution)/shard_map/both1/pallas_call | solution.py:546
  123.8 92.0 %backward0.1 = (bf16[32,1408]{1,0:T(8,128)(2,1)}, bf16[32,1408]{1,0:T(8,128)(2,1)}, bf16[32,1408]{1,0:T(8,128)(2,1)}, bf16[32,1408]{1,0:T(8,128)(2,1)}, bf16[88,...) custom-call(bf16[4096,512]{1,0:T(8,128)(2,1)} %get-tuple-element.29.a, ...), custom_call_target="tpu_custom_call" | custom-call | tf_op jit(solution)/shard_map/backward0/pallas_call | solution.py:579
  215.7 3.8 %adamw.1 = (bf16[2,32,1408]{2,1,0:T(8,128)(2,1)}, bf16[2,32,1408]{2,1,0:T(8,128)(2,1)}, bf16[2,88,512]{2,1,0:T(8,128)(2,1)}, f32[2,32,1408]{2,1,0:T(8,128)}, f32...) custom-call(f32[8,128]{1,0:T(8,128)} %get-tuple-element.42.total, ...), custom_call_target="tpu_custom_call" | custom-call | tf_op jit(solution)/shard_map/adamw/pallas_call | solution.py:593

commit v4 on v2

--- a/solution.py
+++ b/solution.py
@@ -247,8 +247,8 @@
 
 CHUNKS = (512, 512, 384)
 SCHEDULE = {
-    "first": (2, 3, 5, 7, 10),
-    "second": (2, 4, 6, 8, 11),
+    "first": (2, 3, 5, 7),
+    "second": (2, 4, 6, 8),
     "chunk0": (4, 5, 6, 8, 10),
     "chunk1": (8, 9, 11),
 }
@@ -283,18 +283,14 @@
             copy.start()
 
     for step in range(1, last + 1):
-
-        @pl.when(i == step)
-        def _(step=step):
-            for m in pieces:
-                two.step(step, m)
-                if step > 1:
-                    two.crossed(step - 1, m)
-
-    @pl.when(i == last + 1)
-    def _():
-        for m in pieces:
-            two.crossed(last, m)
+        for late, some in enumerate(((0, 1), (2, 3))):
+
+            @pl.when(i == min(2 * step - 1 + late, 2 * last - 1))
+            def _(step=step, some=some):
+                for m in some:
+                    two.step(step, m)
+                    if step > 1:
+                        two.crossed(step - 1, m)
 
     h = x[...]
     _, _, a = norm_parts(h)
@@ -309,6 +305,8 @@
 
     @pl.when(i == n - 1)
     def _():
+        for m in pieces:
+            two.crossed(last, m)
         two.finish()
         for copy in keep:
             copy.wait()
@@ -394,10 +392,9 @@
         return [r.at[:, starts[k] : starts[k] + sizes[k]] for r in (rg, ru)]
 
     events = []
-    for name, scatter, outs in (("first", first, (rg1, ru1)), ("second", second, (rd1, rd0))):
+    for name, scatter in (("first", first), ("second", second)):
         times = SCHEDULE[name]
         events += [(times[s], functools.partial(scatter.step, s)) for s in range(steps)]
-        events.append((times[steps], functools.partial(settle, scatter, outs)))
     for k in range(len(sizes) - 1):
         times = SCHEDULE[f"chunk{k}"]
         for s in range(len(times) - 1):
@@ -447,11 +444,15 @@
     def _():
         done = [len(SCHEDULE[f"chunk{k}"]) - 1 for k in range(len(sizes) - 1)] + [0]
         for s in range(steps):
-            for k, chunk in enumerate(chunks):
+            for k, chunk in reversed(list(enumerate(chunks))):
                 if done[k] <= steps and done[k] + s < steps:
                     chunk.step(done[k] + s)
                 elif done[k] <= steps and done[k] + s == steps:
                     settle(chunk, chunk_outs(k))
+            if s == steps - 2:
+                settle(first, (rg1, ru1))
+            if s == steps - 1:
+                settle(second, (rd1, rd0))
         settle(chunks[-1], chunk_outs(len(sizes) - 1))
         part[...] = squares[...]
         copies = [remote(part, parts.at[group - k - 1], part_send.at[k - 1], part_recv.at[group - k - 1], lax.rem(me + k, group)) for k in range(1, group)]

time: 214 us -> 212 us (level)
  Pallas kernels: 214 us -> 211 us
    pallas_call x1, Pallas kernels: 78.6 us -> 76.5 us  [step(): pl.pallas_call(functools.partial(backward_kernel, chips, tiles, sizes), g...]
where the time goes in v4:
time: 212 us
  Pallas kernels  211 us (100%)
    pallas_call x1, Pallas kernels, step(): pl.pallas_call(functools.partial(backward_kernel, chips, tiles, sizes), g...  76.5 us
    pallas_call x1, Pallas kernels, step(): pl.pallas_call(both_kernel, grid=(tiles,), out_shape=[tokens_d, wide, wid...  71.1 us
    pallas_call x1, Pallas kernels, step(): pl.pallas_call(functools.partial(forward_kernel, chips, groups), grid=(ti...  59.4 us

profile of v4, /device:TPU:21, one launch (start us, length us, event | category | flops | bytes accessed | tf_op | source)
XLA Modules:
  0.0 211.7 jit_solution(3106393028913942558)
XLA Ops:
  0.6 59.4 %forward0.1 = (bf16[4096,512]{1,0:T(8,128)(2,1)}, bf16[4096,1408]{1,0:T(8,128)(2,1)}, bf16[4096,512]{1,0:T(8,128)(2,1)}, bf16[512,4096]{1,0:T(8,128)(2,1)}, bf16...) custom-call(bf16[4096,512]{1,0:T(8,128)(2,1)} %bitcast.10, ...), custom_call_target="tpu_custom_call" | custom-call | tf_op jit(solution)/shard_map/forward0/pallas_call | solution.py:523
  60.1 71.1 %both1.1 = (bf16[4096,512]{1,0:T(8,128)(2,1)}, bf16[512,1408]{1,0:T(8,128)(2,1)}, bf16[512,1408]{1,0:T(8,128)(2,1)}, bf16[1408,512]{1,0:T(8,128)(2,1)}, bf16[1408,512]{1,0:T(8,128)(2,1)}) custom-call(bf16[4096,512]{1,0:T(8,128)(2,1)} %get-tuple-element.31.h, bf16[4096,512]{1,0:T(8,128)(2,1)} %bitcast.11, bf16[4096,1408]{1,0:T(8,128)(2,1)} %get-tuple-element.32.act0, ...), custom_call_target="tpu_custom_call" | custom-call | tf_op jit(solution)/shard_map/both1/pallas_call | solution.py:537
  131.2 76.5 %backward0.1 = (bf16[32,1408]{1,0:T(8,128)(2,1)}, bf16[32,1408]{1,0:T(8,128)(2,1)}, bf16[32,1408]{1,0:T(8,128)(2,1)}, bf16[32,1408]{1,0:T(8,128)(2,1)}, bf16[88,...) custom-call(bf16[4096,512]{1,0:T(8,128)(2,1)} %get-tuple-element.29.a, ...), custom_call_target="tpu_custom_call" | custom-call | tf_op jit(solution)/shard_map/backward0/pallas_call | solution.py:561
  207.6 3.8 %adamw.1 = (bf16[2,32,1408]{2,1,0:T(8,128)(2,1)}, bf16[2,32,1408]{2,1,0:T(8,128)(2,1)}, bf16[2,88,512]{2,1,0:T(8,128)(2,1)}, f32[2,32,1408]{2,1,0:T(8,128)}, f32...) custom-call(f32[8,128]{1,0:T(8,128)} %get-tuple-element.42.total, ...), custom_call_target="tpu_custom_call" | custom-call | tf_op jit(solution)/shard_map/adamw/pallas_call | solution.py:575
